TPU v7x, 1024 devices: a whole 8x8x8 slice. The times are simulated.
1024 devices in a mesh: dp: 16 (over y, z_lo), expert: 16 (over x, core), etp: 4 (over z_hi).
Axes of the slice: x: 8, y: 8, z: 8 (z_hi: 4, z_lo: 2; z = z_hi * 2 + z_lo), core: 2. Of those that a mesh axis runs over, the one named last changes fastest.
Arguments:
- tokens: bfloat16 [16384, 4096], P(('dp', 'expert')), parts along dimension 0, may hold values from -6 to 6
- expert_ids: int32 [16384, 2], P(('dp', 'expert')), parts along dimension 0, may hold values from 0 to 15, all different within a row; in each aligned block of 64 rows (0 to 63, 64 to 127, ...) at most 16 rows name the same one
- route_weights: bfloat16 [16384, 2], P(('dp', 'expert')), parts along dimension 0, may hold values from 0.049804688 to 1
- w_gate: bfloat16 [16, 4096, 1536], P('expert', None, 'etp'), may hold values from -0.09375 to 0.09375
- w_up: bfloat16 [16, 4096, 1536], P('expert', None, 'etp'), may hold values from -0.09375 to 0.09375
- w_down: bfloat16 [16, 1536, 4096], P('expert', 'etp'), may hold values from -0.15625 to 0.15625
Outputs:
- moe_out: bfloat16 [16384, 4096], P(('dp', 'expert'), 'etp'), parts along dimension 0
There are 16 independent parts, one for each index of `dp`. A program takes and returns all parts, laid end to end along the dimension named above; an argument that names none is the same for every part. Nothing has to cross between parts.
Inputs may be any that keep to these rules, and one draw needn't show every extreme that they name: `expert_ids`: within the 64 rows of one index of expert (aligned blocks), a row names 2 different experts and no expert is named by more than 16 rows; some expert is named by exactly 16 rows of some block.
All inputs are finite; a program needn't handle non-finite values.
Results may differ from a plain program's by a relative error of at most 0.01.
Values may be sent and summed in bfloat16 or wider, within the bound.
No kernel may reach another device: no remote copies, remote signals or barrier semaphores. Data moves between devices by JAX's collectives and lax.ppermute only.
A program may use at most 32 MiB of HBM per device.

v0:
```python
import jax
import jax.numpy as jnp
from jax import lax
from jax.sharding import PartitionSpec as P


def split_up(shard, dim, count):
    dims = shard.shape
    blocks = shard.reshape(*dims[:dim], count, dims[dim] // count, *dims[dim + 1 :])
    return jnp.moveaxis(blocks, dim, 0)


def sum_at_owner(shard, axis, dim):
    count = lax.axis_size(axis)
    blocks = lax.all_to_all(split_up(shard, dim, count), axis, 0, 0, tiled=True)
    return jnp.sum(blocks.astype(jnp.float32), axis=0)


def per_device(tokens, expert_ids, route_weights, w_gate, w_up, w_down):
    tok_rows, width = tokens.shape
    route_count = expert_ids.shape[1]
    local_experts = w_gate.shape[0]
    sources = lax.axis_size("expert")
    experts = local_experts * sources
    capacity = 2 * tok_rows * route_count // experts
    quarter = width // lax.axis_size("etp")
    flat_ids = expert_ids.reshape(-1)
    onehot = (flat_ids[:, None] == jnp.arange(experts, dtype=jnp.int32)[None, :]).astype(jnp.int32)
    before = jnp.cumsum(onehot, axis=0) - onehot
    slots = jnp.sum(before * onehot, axis=1)
    position = (flat_ids * capacity + slots).reshape(tok_rows, route_count)
    targets = jnp.arange(experts * capacity, dtype=jnp.int32)
    hits = position[:, :, None] == targets[None, None, :]
    dispatch_map = jnp.transpose(jnp.any(hits, axis=1)).astype(jnp.bfloat16)
    combine_map = jnp.sum(
        jnp.where(hits, route_weights[:, :, None], jnp.zeros((), jnp.bfloat16)), axis=1
    )
    outgoing = jnp.dot(dispatch_map, tokens, preferred_element_type=jnp.float32).astype(
        jnp.bfloat16
    )
    arrived = lax.all_to_all(
        outgoing.reshape(experts, capacity, width),
        "expert",
        split_axis=0,
        concat_axis=0,
        tiled=True,
    )
    arrived = arrived.reshape(sources, local_experts, capacity, width)
    gate = jnp.einsum("secd,edh->sech", arrived, w_gate, preferred_element_type=jnp.float32)
    up = jnp.einsum("secd,edh->sech", arrived, w_up, preferred_element_type=jnp.float32)
    hidden = (jax.nn.silu(gate) * up).astype(jnp.bfloat16)
    partial_out = jnp.einsum("sech,ehd->secd", hidden, w_down, preferred_element_type=jnp.float32)
    partial_out = partial_out.reshape(sources * local_experts, capacity, width)
    summed = sum_at_owner(partial_out.astype(jnp.bfloat16), "etp", 2).astype(jnp.bfloat16)
    returned = lax.all_to_all(summed, "expert", split_axis=0, concat_axis=0, tiled=True)
    mixed = jnp.dot(
        combine_map,
        returned.reshape(experts * capacity, quarter),
        preferred_element_type=jnp.float32,
    )
    return mixed.astype(jnp.bfloat16)


def solution(mesh):
    return jax.shard_map(
        per_device,
        mesh=mesh,
        in_specs=(
            P(("dp", "expert"), None),
            P(("dp", "expert"), None),
            P(("dp", "expert"), None),
            P("expert", None, "etp"),
            P("expert", None, "etp"),
            P("expert", "etp", None),
        ),
        out_specs=P(("dp", "expert"), "etp"),
        check_vma=False,
    )
```

profile of v0, /device:TPU:1, one launch (start us, length us, event | category | flops | bytes accessed | tf_op | source)
XLA Modules:
  0.0 170.4 jit_solution(10884345020339294977)
XLA Ops:
  0.0 0.0 copy-start
  0.0 0.9 copy.25
  0.9 0.1 eq.28
  1.1 0.1 fusion.32
  1.2 0.2 reduce_window_sum.11
  1.3 0.2 select_reduce_fusion
  1.5 0.1 reduce_sum.36
  1.7 0.1 copy.26
  1.7 0.7 multiply_add_fusion
  2.4 0.1 fusion.29
  2.5 0.0 copy-start.3
  2.5 1.9 %convolution_convert_fusion.1 = bf16[256,4096]{1,0:T(8,128)(2,1)S(1)} fusion(pred[64,256]{1,0:T(8,128)(4,1)S(1)} %fusion.29, bf16[64,4096]{1,0:T(8,128)(2,1)} %param.6), kind=kOutput, calls=%fused_computation.1 | convolution fusion | flops 135266304 | bytes 2637824 | tf_op jit(solution)/shard_map/dot_general | solution.py:38
  4.5 67.6 %all_to_all.15 = bf16[16,16,4096]{2,1,0:T(8,128)(2,1)S(1)} all-to-all(bf16[16,16,4096]{2,1,0:T(8,128)(2,1)S(1)} %bitcast.69), channel_id=1, replica_groups=mesh['dp'=16,'expert'=16,'etp'=4] {'expert'}, dimensions={0} | all-to-all | bytes 4194304 | tf_op jit(solution)/shard_map/all_to_all | solution.py:41
  72.1 0.0 copy-start.1
  72.1 1.3 copy-done.1
  73.3 0.0 copy-done.3
  73.3 2.1 %fusion.6 = f32[16,1,16,384]{3,2,0,1:T(8,128)} fusion(bf16[16,16,4096]{2,1,0:T(8,128)(2,1)S(1)} %all_to_all.15, bf16[1,4096,384]{2,1,0:T(8,128)(2,1)S(1)} %copy-done.3), kind=kOutput, calls=%fused_computation.9 | convolution fusion | flops 805306368 | bytes 5636096 | tf_op jit(solution)/shard_map/secd,edh->sech/dot_general | solution.py:49
  75.4 0.0 copy-done
  75.4 6.4 %fusion = bf16[16,1,16,4096]{3,2,0,1:T(8,128)(2,1)} fusion(bf16[1,384,4096]{2,1,0:T(8,128)(2,1)S(1)} %copy-done, bf16[16,16,4096]{2,1,0:T(8,128)(2,1)} %copy-done.1, bf16[1,4096,384]{2,1,0:T(8,128)(2,1)} %param.10, f32[16,1,16,384]{3,2,0,1:T(8,128)} %fusion.6), kind=kOutput, calls=%fused_computation.2 | convolution fusion | flops 1612251136 | bytes 10878976 | tf_op jit(solution)/shard_map/sech,ehd->secd/dot_general | solution.py:52
  81.8 4.5 %convert_element_type.40 = bf16[16,16,4,1024]{3,2,1,0:T(4,128)(2,1)} reshape(bf16[16,1,16,4096]{3,2,0,1:T(8,128)(2,1)} %fusion) | data formatting | bytes 4194304 | tf_op jit(solution)/shard_map/convert_element_type | solution.py:54
  86.3 2.2 %copy.29 = bf16[16,16,4,1024]{3,1,0,2:T(8,128)(2,1)S(1)} copy(bf16[16,16,4,1024]{3,2,1,0:T(4,128)(2,1)} %convert_element_type.40) | data formatting | bytes 4194304 | tf_op jit(solution)/shard_map/convert_element_type | solution.py:54
  88.5 0.0 copy-start.2
  88.5 57.8 %all_to_all.16 = bf16[4,16,16,1024]{3,2,1,0:T(8,128)(2,1)} all-to-all(bf16[4,16,16,1024]{3,2,1,0:T(8,128)(2,1)S(1)} %bitcast.70), channel_id=1, replica_groups=mesh['dp'=16,'expert'=16,'etp'=4] {'etp'}, dimensions={0} | all-to-all | bytes 4194304 | tf_op jit(solution)/shard_map/all_to_all | solution.py:15
  146.3 2.9 %reduce_sum.38 = bf16[16,16,1024]{2,1,0:T(8,128)(2,1)} reduce(bf16[4,16,16,1024]{3,2,1,0:T(8,128)(2,1)} %all_to_all.16, bf16[]{:T(256)} %constant.15.clone.1), dimensions={0}, to_apply=%region_4.5 | reduce | flops 786432 | bytes 2621442 | tf_op jit(solution)/shard_map/reduce_sum | solution.py:16
  149.3 4.1 %all-to-all-start.2 = ((bf16[16,16,1024]{2,1,0:T(8,128)(2,1)}), bf16[16,16,1024]{2,1,0:T(8,128)(2,1)}, u32[]{:S(2)}, u32[]{:S(2)}) async-start(bf16[16,16,1024]{2,1,0:T(8,128)(2,1)} %reduce_sum.38), calls=%async_computation.2 | async-start | bytes 1048576 | tf_op jit(solution)/shard_map/all_to_all | solution.py:55
  153.4 0.0 copy-done.2
  153.4 0.1 fusion.31
  153.5 14.9 %all-to-all-done.2 = bf16[16,16,1024]{2,1,0:T(8,128)(2,1)} async-done(((bf16[16,16,1024]{2,1,0:T(8,128)(2,1)}), bf16[16,16,1024]{2,1,0:T(8,128)(2,1)}, u32[]{:S(2)}, u32[]{:S(2)}) %all-to-all-start.2) | async-done | bytes 524320 | tf_op jit(solution)/shard_map/all_to_all | solution.py:55
  168.5 1.9 %convolution_convert_fusion.2 = bf16[64,1024]{1,0:T(8,128)(2,1)} fusion(bf16[64,256]{1,0:T(8,128)(2,1)S(1)} %fusion.31, bf16[256,1024]{1,0:T(8,128)(2,1)} %bitcast.20), kind=kOutput, calls=%fused_computation.13 | convolution fusion | flops 33619968 | bytes 688128 | tf_op jit(solution)/shard_map/dot_general | solution.py:56
Async XLA Ops:
  0.0 75.4 %copy-start = (bf16[1,384,4096]{2,1,0:T(8,128)(2,1)S(1)}, bf16[1,384,4096]{2,1,0:T(8,128)(2,1)}, u32[]{:S(2)}) copy-start(bf16[1,384,4096]{2,1,0:T(8,128)(2,1)} %param.11) | copy-start | bytes 9437188
  2.5 70.8 %copy-start.3 = (bf16[1,4096,384]{2,1,0:T(8,128)(2,1)S(1)}, bf16[1,4096,384]{2,1,0:T(8,128)(2,1)}, u32[]{:S(2)}) copy-start(bf16[1,4096,384]{2,1,0:T(8,128)(2,1)} %param.9) | copy-start | bytes 9437188
  72.1 1.3 copy-start.1
  88.5 64.9 %copy-start.2 = (bf16[64,2]{0,1:T(2,128)(2,1)S(1)}, bf16[64,2]{0,1:T(2,128)(2,1)}, u32[]{:S(2)}) copy-start(bf16[64,2]{0,1:T(2,128)(2,1)} %param.8) | copy-start | bytes 772
  149.3 19.2 %all-to-all-start.2 = ((bf16[16,16,1024]{2,1,0:T(8,128)(2,1)}), bf16[16,16,1024]{2,1,0:T(8,128)(2,1)}, u32[]{:S(2)}, u32[]{:S(2)}) async-start(bf16[16,16,1024]{2,1,0:T(8,128)(2,1)} %reduce_sum.38), calls=%async_computation.2 | async-start | bytes 1048576 | tf_op jit(solution)/shard_map/all_to_all | solution.py:55
where the time goes:
time: 171 us; the launch traced here: 170 us
  blocking collectives  125 us (73%)
  waiting for transfers between devices  14.9 us (9%)
  matrix products  12.3 us (7%)
  local copies, waits for them, and re-layouts  9.3 us (5%)
  other arithmetic  4.25 us (2%)
  starting transfers between devices  4.13 us (2%)
    all_to_all x1, blocking collectives, per_device(): lax.all_to_all(outgoing.reshape(experts, capacity, width), 'expert', spli...  67.6 us
    all_to_all x1, blocking collectives, sum_at_owner(): blocks = lax.all_to_all(split_up(shard, dim, count), axis, 0, 0, tiled=True)  57.8 us
    all_to_all x1, waiting for transfers between devices, per_device(): lax.all_to_all(summed, 'expert', split_axis=0, concat_axis=0, tiled=True)  14.9 us
    convert_element_type x2, local copies, waits for them, and re-layouts, per_device(): partial_out.astype(jnp.bfloat16)  6.73 us
    dot_general x1, matrix products, per_device(): jnp.einsum('sech,ehd->secd', hidden, w_down, preferred_element_type=jnp.f...  6.37 us
    all_to_all x1, starting transfers between devices, per_device(): lax.all_to_all(summed, 'expert', split_axis=0, concat_axis=0, tiled=True)  4.13 us
  transfers between devices with their start and end apart: 1, of which 1 were waited for; matrix products, arithmetic and copies ran while one was open for 0% of the time, Pallas kernels for 0%

commit v1 on v0

v1 whole, which is shorter than its diff:
```python
import jax
import jax.numpy as jnp
from jax import lax
from jax.experimental import pallas as pl
from jax.experimental.pallas import tpu as pltpu
from jax.sharding import PartitionSpec as P

def ffn_kernel(x_ref, gate_ref, up_ref, down_ref, out_ref, down_buf, sems):
    sources, quarters, capacity, part = out_ref.shape
    copies = [
        pltpu.make_async_copy(
            down_ref.at[:, pl.ds(q * part, part)], down_buf.at[:, pl.ds(q * part, part)], sems.at[q]
        )
        for q in range(quarters)
    ]
    for copy in copies:
        copy.start()
    x = x_ref[...]
    gate = jnp.dot(x, gate_ref[...], preferred_element_type=jnp.float32)
    up = jnp.dot(x, up_ref[...], preferred_element_type=jnp.float32)
    hidden = (gate / (1.0 + jnp.exp(-gate)) * up).astype(jnp.bfloat16)
    for q in range(quarters):
        copies[q].wait()
        out = jnp.dot(hidden, down_buf[:, pl.ds(q * part, part)], preferred_element_type=jnp.float32)
        out_ref[:, q] = out.astype(out_ref.dtype).reshape(sources, capacity, part)


def ffn(arrived, w_gate, w_up, w_down, sources, quarters):
    rows, width = arrived.shape
    hidden_units = w_gate.shape[1]
    in_vmem = pl.BlockSpec(memory_space=pltpu.VMEM)
    return pl.pallas_call(
        ffn_kernel,
        out_shape=jax.ShapeDtypeStruct(
            (sources, quarters, rows // sources, width // quarters), jnp.bfloat16
        ),
        in_specs=[in_vmem, in_vmem, in_vmem, pl.BlockSpec(memory_space=pltpu.HBM)],
        out_specs=in_vmem,
        scratch_shapes=[
            pltpu.VMEM((hidden_units, width), jnp.bfloat16),
            pltpu.SemaphoreType.DMA((quarters,)),
        ],
        compiler_params=pltpu.CompilerParams(vmem_limit_bytes=32 * 2**20),
        cost_estimate=pl.CostEstimate(
            flops=6 * rows * width * hidden_units,
            bytes_accessed=2 * (2 * rows * width + 3 * width * hidden_units),
            transcendentals=rows * hidden_units,
        ),
    )(arrived, w_gate, w_up, w_down)


def per_device(tokens, expert_ids, route_weights, w_gate, w_up, w_down):
    tok_rows, width = tokens.shape
    route_count = expert_ids.shape[1]
    sources = lax.axis_size("expert")
    quarters = lax.axis_size("etp")
    experts = sources
    capacity = 2 * tok_rows * route_count // experts
    quarter = width // quarters
    flat_ids = expert_ids.reshape(-1)
    onehot = (flat_ids[:, None] == jnp.arange(experts, dtype=jnp.int32)[None, :]).astype(jnp.int32)
    before = jnp.cumsum(onehot, axis=0) - onehot
    slots = jnp.sum(before * onehot, axis=1)
    position = (flat_ids * capacity + slots).reshape(tok_rows, route_count)
    targets = jnp.arange(experts * capacity, dtype=jnp.int32)
    hits = position[:, :, None] == targets[None, None, :]
    dispatch_map = jnp.transpose(jnp.any(hits, axis=1)).astype(jnp.bfloat16)
    outgoing = jnp.dot(dispatch_map, tokens, preferred_element_type=jnp.float32).astype(
        jnp.bfloat16
    )
    arrived = lax.all_to_all(
        outgoing.reshape(experts, capacity, width),
        "expert",
        split_axis=0,
        concat_axis=0,
        tiled=True,
    )
    partial_out = ffn(
        arrived.reshape(sources * capacity, width), w_gate[0], w_up[0], w_down[0], sources, quarters
    )
    returned = lax.all_to_all(
        partial_out.reshape(sources * quarters, capacity, quarter),
        ("expert", "etp"),
        split_axis=0,
        concat_axis=0,
        tiled=True,
    )
    row = jnp.arange(experts * quarters * capacity, dtype=jnp.int32)
    place = row // (quarters * capacity) * capacity + row % capacity
    spread = position[:, :, None] == place[None, None, :]
    combine_map = jnp.sum(
        jnp.where(spread, route_weights[:, :, None], jnp.zeros((), jnp.bfloat16)), axis=1
    )
    mixed = jnp.dot(
        combine_map,
        returned.reshape(experts * quarters * capacity, quarter),
        preferred_element_type=jnp.float32,
    )
    return mixed.astype(jnp.bfloat16)


def solution(mesh):
    return jax.shard_map(
        per_device,
        mesh=mesh,
        in_specs=(
            P(("dp", "expert"), None),
            P(("dp", "expert"), None),
            P(("dp", "expert"), None),
            P("expert", None, "etp"),
            P("expert", None, "etp"),
            P("expert", "etp", None),
        ),
        out_specs=P(("dp", "expert"), "etp"),
        check_vma=False,
    )
```

time: 171 us -> 140 us (0.82)
  blocking collectives: 125 us -> 67.8 us
  waiting for transfers between devices: 14.9 us -> 50.9 us
  matrix products: 12.3 us -> 1.88 us
  local copies, waits for them, and re-layouts: 9.3 us -> 3.09 us
  Pallas kernels: 0 us -> 5.86 us
  starting transfers between devices: 4.13 us -> 8.85 us
  other arithmetic: 4.25 us -> 1.35 us
    all_to_all x1 -> x0, blocking collectives: 57.8 us -> none  [sum_at_owner(): blocks = lax.all_to_all(split_up(shard, dim, count), axis, 0, 0, tiled=True)]
    all_to_all x1, waiting for transfers between devices: 14.9 us -> 50.9 us  [per_device(): lax.all_to_all(partial_out.reshape(sources * quarters, capacity, quarter)...]
    dot_general x3 -> x1, matrix products: 10.3 us -> 1.14 us  [per_device(): jnp.dot(combine_map, returned.reshape(experts * quarters * capacity, quar...]
    convert_element_type x2 -> x0, local copies, waits for them, and re-layouts: 6.73 us -> none  [per_device(): partial_out.astype(jnp.bfloat16)]
    pallas_call x0 -> x1, Pallas kernels: none -> 5.86 us  [ffn(): pl.pallas_call(ffn_kernel, out_shape=jax.ShapeDtypeStruct((sources, quart...]
    all_to_all x1, starting transfers between devices: 4.13 us -> 8.85 us  [per_device(): lax.all_to_all(partial_out.reshape(sources * quarters, capacity, quarter)...]
    reduce_sum x2 -> x1, other arithmetic: 3.04 us -> 0.13 us  [per_device(): jnp.sum(jnp.where(spread, route_weights[:, :, None], jnp.zeros((), jnp.bf...]
where the time goes in v1:
time: 140 us
  blocking collectives  67.8 us (48%)
  waiting for transfers between devices  50.9 us (36%)
  starting transfers between devices  8.85 us (6%)
  Pallas kernels  5.86 us (4%)
  local copies, waits for them, and re-layouts  3.09 us (2%)
  matrix products  1.88 us (1%)
    all_to_all x1, blocking collectives, per_device(): lax.all_to_all(outgoing.reshape(experts, capacity, width), 'expert', spli...  67.8 us
    all_to_all x1, waiting for transfers between devices, per_device(): lax.all_to_all(partial_out.reshape(sources * quarters, capacity, quarter)...  50.9 us
    all_to_all x1, starting transfers between devices, per_device(): lax.all_to_all(partial_out.reshape(sources * quarters, capacity, quarter)...  8.85 us
    pallas_call x1, Pallas kernels, ffn(): pl.pallas_call(ffn_kernel, out_shape=jax.ShapeDtypeStruct((sources, quart...  5.86 us
  transfers between devices with their start and end apart: 1, of which 1 were waited for; matrix products, arithmetic and copies ran while one was open for 0% of the time, Pallas kernels for 0%

profile of v1, /device:TPU:1, one launch (start us, length us, event | category | flops | bytes accessed | tf_op | source)
XLA Modules:
  0.0 139.8 jit_solution(17768464511158055199)
XLA Ops:
  0.0 0.0 copy-start
  0.0 0.8 copy.20
  0.8 0.1 eq.22
  1.0 0.1 fusion.2
  1.1 0.2 reduce_window_sum.11
  1.2 0.2 select_reduce_fusion
  1.4 0.1 reduce_sum.24
  1.6 0.1 copy.21
  1.6 0.7 multiply_add_fusion
  2.3 0.1 fusion.1
  2.4 0.0 copy-done
  2.4 0.0 copy-start.2
  2.4 0.7 convolution_convert_fusion
  3.2 0.0 copy-start.1
  3.2 67.8 %all_to_all.10 = bf16[16,16,4096]{2,1,0:T(8,128)(2,1)S(1)} all-to-all(bf16[16,16,4096]{2,1,0:T(8,128)(2,1)S(1)} %bitcast.15), channel_id=1, replica_groups=mesh['dp'=16,'expert'=16,'etp'=4] {'expert'}, dimensions={0} | all-to-all | bytes 4194304 | tf_op jit(solution)/shard_map/all_to_all | solution.py:71
  71.1 0.0 copy-done.2
  71.1 0.0 copy-done.1
  71.1 0.0 copy-start.3
  71.1 1.9 %copy-done.3 = bf16[1,384,4096]{2,1,0:T(8,128)(2,1)S(1)} copy-done((bf16[1,384,4096]{2,1,0:T(8,128)(2,1)S(1)}, bf16[1,384,4096]{2,1,0:T(8,128)(2,1)}, u32[]{:S(2)}) %copy-start.3) | copy-done | bytes 3145752
  72.9 5.9 %shard_map.64 = bf16[16,4,16,1024]{3,2,1,0:T(8,128)(2,1)} custom-call(bf16[256,4096]{1,0:T(8,128)(2,1)S(1)} %bitcast.11, bf16[4096,384]{1,0:T(8,128)(2,1)S(1)} %bitcast.12, bf16[4096,384]{1,0:T(8,128)(2,1)S(1)} %bitcast.13, bf16[384,4096]{1,0:T(8,128)(2,1)S(1)} %bitcast.14), custom_call_target="tpu_custom_call" | custom-call | flops 2415919104 | bytes 13631488 | tf_op jit(solution)/shard_map/pallas_call | solution.py:32
  78.8 0.0 copy-start.4
  78.8 8.8 %all-to-all-start.1 = ((bf16[64,16,1024]{2,1,0:T(8,128)(2,1)}), bf16[64,16,1024]{2,1,0:T(8,128)(2,1)S(1)}, u32[]{:S(2)}, u32[]{:S(2)}) async-start(bf16[64,16,1024]{2,1,0:T(8,128)(2,1)} %bitcast.5), calls=%async_computation.1 | async-start | bytes 4194304 | tf_op jit(solution)/shard_map/all_to_all | solution.py:81
  87.7 0.0 copy-done.4
  87.7 0.1 fusion
  87.8 50.9 %all-to-all-done.1 = bf16[64,16,1024]{2,1,0:T(8,128)(2,1)S(1)} async-done(((bf16[64,16,1024]{2,1,0:T(8,128)(2,1)}), bf16[64,16,1024]{2,1,0:T(8,128)(2,1)S(1)}, u32[]{:S(2)}, u32[]{:S(2)}) %all-to-all-start.1) | async-done | bytes 2097184 | tf_op jit(solution)/shard_map/all_to_all | solution.py:81
  138.7 1.1 convolution_convert_fusion.1
  (1 shorter events, 0.0 us)
Async XLA Ops:
  0.0 2.4 %copy-start = (bf16[64,4096]{1,0:T(8,128)(2,1)S(1)}, bf16[64,4096]{1,0:T(8,128)(2,1)}, u32[]{:S(2)}) copy-start(bf16[64,4096]{1,0:T(8,128)(2,1)} %param.6) | copy-start | bytes 1572868
  2.4 68.6 %copy-start.2 = (bf16[1,4096,384]{2,1,0:T(8,128)(2,1)S(1)}, bf16[1,4096,384]{2,1,0:T(8,128)(2,1)}, u32[]{:S(2)}) copy-start(bf16[1,4096,384]{2,1,0:T(8,128)(2,1)} %param.10) | copy-start | bytes 9437188
  3.2 67.9 %copy-start.1 = (bf16[1,4096,384]{2,1,0:T(8,128)(2,1)S(1)}, bf16[1,4096,384]{2,1,0:T(8,128)(2,1)}, u32[]{:S(2)}) copy-start(bf16[1,4096,384]{2,1,0:T(8,128)(2,1)} %param.9) | copy-start | bytes 9437188
  71.1 1.9 %copy-start.3 = (bf16[1,384,4096]{2,1,0:T(8,128)(2,1)S(1)}, bf16[1,384,4096]{2,1,0:T(8,128)(2,1)}, u32[]{:S(2)}) copy-start(bf16[1,384,4096]{2,1,0:T(8,128)(2,1)} %param.11) | copy-start | bytes 9437188
  78.8 8.9 %copy-start.4 = (bf16[64,2]{0,1:T(2,128)(2,1)S(1)}, bf16[64,2]{0,1:T(2,128)(2,1)}, u32[]{:S(2)}) copy-start(bf16[64,2]{0,1:T(2,128)(2,1)} %param.8) | copy-start | bytes 772
  78.8 59.9 %all-to-all-start.1 = ((bf16[64,16,1024]{2,1,0:T(8,128)(2,1)}), bf16[64,16,1024]{2,1,0:T(8,128)(2,1)S(1)}, u32[]{:S(2)}, u32[]{:S(2)}) async-start(bf16[64,16,1024]{2,1,0:T(8,128)(2,1)} %bitcast.5), calls=%async_computation.1 | async-start | bytes 4194304 | tf_op jit(solution)/shard_map/all_to_all | solution.py:81

commit v2 on v0

v2 whole, which is shorter than its diff:
```python
import jax
import jax.numpy as jnp
from jax import lax
from jax.experimental import pallas as pl
from jax.experimental.pallas import tpu as pltpu
from jax.sharding import PartitionSpec as P


DP_STEP = 2


def shift(x, axis, by):
    count = lax.axis_size(axis)
    return lax.ppermute(x, axis, [(i, (i + by) % count) for i in range(count)])


STEPS = 4


def hidden_kernel(x_ref, gate_ref, up_ref, out_ref, x_buf, gate_buf, up_buf, sems):
    rows, width = x_ref.shape
    depth = width // STEPS
    copies = []
    for k in range(STEPS):
        part = pl.ds(k * depth, depth)
        copies.append(
            (
                pltpu.make_async_copy(x_ref.at[:, part], x_buf.at[:, part], sems.at[0, k]),
                pltpu.make_async_copy(gate_ref.at[part], gate_buf.at[part], sems.at[1, k]),
                pltpu.make_async_copy(up_ref.at[part], up_buf.at[part], sems.at[2, k]),
            )
        )
    for group in copies:
        for copy in group:
            copy.start()
    gate = jnp.zeros((rows, gate_ref.shape[1]), jnp.float32)
    up = jnp.zeros((rows, gate_ref.shape[1]), jnp.float32)
    for k in range(STEPS):
        for copy in copies[k]:
            copy.wait()
        part = pl.ds(k * depth, depth)
        x = x_buf[:, part]
        gate += jnp.dot(x, gate_buf[part, :], preferred_element_type=jnp.float32)
        up += jnp.dot(x, up_buf[part, :], preferred_element_type=jnp.float32)
    out_ref[...] = (gate / (1.0 + jnp.exp(-gate)) * up).astype(out_ref.dtype)


def hidden_units(arrived, w_gate, w_up):
    rows, width = arrived.shape
    units = w_gate.shape[1]
    in_vmem = pl.BlockSpec(memory_space=pltpu.VMEM)
    in_hbm = pl.BlockSpec(memory_space=pltpu.HBM)
    return pl.pallas_call(
        hidden_kernel,
        out_shape=jax.ShapeDtypeStruct((rows, units), jnp.bfloat16),
        in_specs=[in_hbm, in_hbm, in_hbm],
        out_specs=in_vmem,
        scratch_shapes=[
            pltpu.VMEM((rows, width), jnp.bfloat16),
            pltpu.VMEM((width, units), jnp.bfloat16),
            pltpu.VMEM((width, units), jnp.bfloat16),
            pltpu.SemaphoreType.DMA((3, STEPS)),
        ],
        compiler_params=pltpu.CompilerParams(vmem_limit_bytes=56 * 2**20),
        cost_estimate=pl.CostEstimate(
            flops=4 * rows * width * units,
            bytes_accessed=2 * (rows * width + 2 * width * units + rows * units),
            transcendentals=rows * units,
        ),
    )(arrived, w_gate, w_up)


def down_kernel(*refs):
    out_ref = refs[-1]
    groups = (len(refs) - 4) // 2
    hidden, own, fetched = refs[: groups + 1], refs[groups + 1], refs[groups + 2 : -3]
    others = refs[-3:-1]
    units = own.shape[0]
    half, piece = fetched[0].shape[1], others[0].shape[1]
    odd = lax.rem(lax.div(lax.axis_index("dp"), DP_STEP), 2)

    def project(start, columns, blocks):
        start = pl.multiple_of(start, piece)
        total = jnp.dot(hidden[0][...], own[:, pl.ds(start, columns)], preferred_element_type=jnp.float32)
        for k in range(groups):
            total += jnp.dot(hidden[k + 1][...], blocks(k), preferred_element_type=jnp.float32)
        out_ref[:, pl.ds(start, columns)] = total.astype(out_ref.dtype)

    project(odd * half, half, lambda k: fetched[k][...])
    for side in range(2):
        project(
            (1 - odd) * half + side * piece,
            piece,
            lambda k: others[side][pl.ds(k * units, units), :],
        )


def project_down(hidden, own, fetched, others):
    rows, units = hidden[0].shape
    quarter = own.shape[1]
    in_vmem = pl.BlockSpec(memory_space=pltpu.VMEM)
    operands = (*hidden, own, *fetched, *others)
    return pl.pallas_call(
        down_kernel,
        out_shape=jax.ShapeDtypeStruct((rows, quarter), jnp.bfloat16),
        in_specs=[in_vmem] * len(operands),
        out_specs=in_vmem,
        compiler_params=pltpu.CompilerParams(vmem_limit_bytes=24 * 2**20),
        cost_estimate=pl.CostEstimate(
            flops=2 * len(hidden) * rows * units * quarter,
            bytes_accessed=2 * len(hidden) * (rows * units + units * quarter) + 2 * rows * quarter,
            transcendentals=0,
        ),
    )(*operands)


def down_weights(w_down, quarter, quarters):
    here = lax.axis_index("etp")
    odd = (lax.axis_index("dp") // DP_STEP) % 2
    half, units = quarter // 2, w_down.shape[0]
    own = lax.dynamic_slice(w_down, (0, here * quarter), (units, quarter))
    parts = [
        lax.dynamic_slice(w_down, (0, (here + k) % quarters * quarter + odd * half), (units, half))
        for k in range(1, quarters)
    ]
    fetched = [shift(part, "etp", k) for k, part in enumerate(parts, 1)]
    stacked = jnp.concatenate(fetched, axis=0)
    others = (
        shift(stacked[:, : half // 2], "dp", DP_STEP),
        shift(stacked[:, half // 2 :], "dp", -DP_STEP),
    )
    return own, fetched, others


def per_device(tokens, expert_ids, route_weights, w_gate, w_up, w_down):
    tok_rows, width = tokens.shape
    route_count = expert_ids.shape[1]
    sources = lax.axis_size("expert")
    quarters = lax.axis_size("etp")
    experts = sources
    capacity = 2 * tok_rows * route_count // experts
    quarter = width // quarters
    flat_ids = expert_ids.reshape(-1)
    onehot = (flat_ids[:, None] == jnp.arange(experts, dtype=jnp.int32)[None, :]).astype(jnp.int32)
    before = jnp.cumsum(onehot, axis=0) - onehot
    slots = jnp.sum(before * onehot, axis=1)
    position = (flat_ids * capacity + slots).reshape(tok_rows, route_count)
    targets = jnp.arange(experts * capacity, dtype=jnp.int32)
    hits = position[:, :, None] == targets[None, None, :]
    dispatch_map = jnp.transpose(jnp.any(hits, axis=1)).astype(jnp.bfloat16)
    combine_map = jnp.sum(
        jnp.where(hits, route_weights[:, :, None], jnp.zeros((), jnp.bfloat16)), axis=1
    )
    outgoing = jnp.dot(dispatch_map, tokens, preferred_element_type=jnp.float32).astype(
        jnp.bfloat16
    )
    arrived = lax.all_to_all(
        outgoing.reshape(experts, capacity, width), "expert", split_axis=0, concat_axis=0, tiled=True
    )
    own, fetched, others = down_weights(w_down[0], quarter, quarters)
    hidden = hidden_units(arrived.reshape(sources * capacity, width), w_gate[0], w_up[0])
    gathered = [hidden] + [shift(hidden, "etp", k) for k in range(1, quarters)]
    expert_out = project_down(gathered, own, fetched, others)
    returned = lax.all_to_all(
        expert_out.reshape(sources, capacity, quarter), "expert", split_axis=0, concat_axis=0, tiled=True
    )
    mixed = jnp.dot(
        combine_map,
        returned.reshape(experts * capacity, quarter),
        preferred_element_type=jnp.float32,
    )
    return mixed.astype(jnp.bfloat16)


def solution(mesh):
    return jax.shard_map(
        per_device,
        mesh=mesh,
        in_specs=(
            P(("dp", "expert"), None),
            P(("dp", "expert"), None),
            P(("dp", "expert"), None),
            P("expert", None, "etp"),
            P("expert", None, "etp"),
            P("expert", "etp", None),
        ),
        out_specs=P(("dp", "expert"), "etp"),
        check_vma=False,
    )
```

time: 171 us -> 137 us (0.80)
  blocking collectives: 125 us -> 0 us
  starting transfers between devices: 4.13 us -> 58.6 us
  waiting for transfers between devices: 14.9 us -> 60.3 us
  matrix products: 12.3 us -> 2.91 us
  Pallas kernels: 0 us -> 8.61 us
  local copies, waits for them, and re-layouts: 9.3 us -> 4.86 us
  other arithmetic: 4.25 us -> 1.32 us
    all_to_all x2 -> x0, blocking collectives: 125 us -> none  [the longest x1 67.6 us: per_device(): lax.all_to_all(outgoing.reshape(experts, capacity, width), 'expert', spli...]
    ppermute x0 -> x8, waiting for transfers between devices: none -> 43.2 us  [shift(): return lax.ppermute(x, axis, [(i, (i + by) % count) for i in range(count)])]
    ppermute x0 -> x8, starting transfers between devices: none -> 31 us  [shift(): return lax.ppermute(x, axis, [(i, (i + by) % count) for i in range(count)])]
    all_to_all x1 -> x2, starting transfers between devices: 4.13 us -> 27.6 us  [the longest x1 18.3 us: per_device(): lax.all_to_all(outgoing.reshape(experts, capacity, width), 'expert', spli...]
    pallas_call x0 -> x2, Pallas kernels: none -> 8.61 us  [the longest x1 5.65 us: hidden_units(): pl.pallas_call(hidden_kernel, out_shape=jax.ShapeDtypeStruct((rows, units...]
    dot_general x2 -> x0, matrix products: 8.42 us -> none  [the longest x1 6.37 us: per_device(): jnp.einsum('sech,ehd->secd', hidden, w_down, preferred_element_type=jnp.f...]
    convert_element_type x2 -> x0, local copies, waits for them, and re-layouts: 6.73 us -> none  [per_device(): partial_out.astype(jnp.bfloat16)]
    reduce_sum x1 -> x0, other arithmetic: 2.94 us -> none  [sum_at_owner(): return jnp.sum(blocks.astype(jnp.float32), axis=0)]
  transfers between devices with their start and end apart: 1 -> 10, of which waited for: 1 -> 6; matrix products, arithmetic and copies ran while one was open for 0% -> 3% of each run, Pallas kernels for 0% -> 4%
where the time goes in v2:
time: 137 us
  waiting for transfers between devices  60.3 us (44%)
  starting transfers between devices  58.6 us (43%)
  Pallas kernels  8.61 us (6%)
  local copies, waits for them, and re-layouts  4.86 us (4%)
  matrix products  2.91 us (2%)
    ppermute x8, waiting for transfers between devices, shift(): return lax.ppermute(x, axis, [(i, (i + by) % count) for i in range(count)])  43.2 us
    ppermute x8, starting transfers between devices, shift(): return lax.ppermute(x, axis, [(i, (i + by) % count) for i in range(count)])  31 us
    all_to_all x1, starting transfers between devices, per_device(): lax.all_to_all(outgoing.reshape(experts, capacity, width), 'expert', spli...  18.3 us
    all_to_all x1, waiting for transfers between devices, per_device(): lax.all_to_all(expert_out.reshape(sources, capacity, quarter), 'expert',...  17.1 us
    all_to_all x1, starting transfers between devices, per_device(): lax.all_to_all(expert_out.reshape(sources, capacity, quarter), 'expert',...  9.35 us
    pallas_call x1, Pallas kernels, hidden_units(): pl.pallas_call(hidden_kernel, out_shape=jax.ShapeDtypeStruct((rows, units...  5.65 us
    pallas_call x1, Pallas kernels, project_down(): pl.pallas_call(down_kernel, out_shape=jax.ShapeDtypeStruct((rows, quarter...  2.96 us
  transfers between devices with their start and end apart: 10, of which 6 were waited for; matrix products, arithmetic and copies ran while one was open for 3% of the time, Pallas kernels for 4%

profile of v2, /device:TPU:1, one launch (start us, length us, event | category | flops | bytes accessed | tf_op | source)
XLA Modules:
  0.0 136.7 jit_solution(11905821737742958242)
XLA Ops:
  0.0 0.0 copy-start
  0.0 0.8 copy.19
  0.8 0.1 eq.33
  1.0 0.1 fusion.3
  1.1 0.2 reduce_window_sum.11
  1.2 0.2 select_reduce_fusion
  1.4 0.1 reduce_sum.24
  1.6 0.1 copy.20
  1.6 0.7 multiply_add_fusion
  2.3 0.1 fusion
  2.4 0.0 copy-done
  2.4 2.0 %convolution_convert_fusion = bf16[256,4096]{1,0:T(8,128)(2,1)} fusion(pred[64,256]{1,0:T(8,128)(4,1)S(1)} %fusion, bf16[64,4096]{1,0:T(8,128)(2,1)S(1)} %copy-done), kind=kOutput, calls=%fused_computation | convolution fusion | flops 135266304 | bytes 2637824 | tf_op jit(solution)/shard_map/dot_general | solution.py:154
  4.5 18.3 %all-to-all-start = ((bf16[16,16,4096]{2,1,0:T(8,128)(2,1)}), bf16[16,16,4096]{2,1,0:T(8,128)(2,1)}, u32[]{:S(2)}, u32[]{:S(2)}) async-start(bf16[16,16,4096]{2,1,0:T(8,128)(2,1)} %bitcast), calls=%async_computation | async-start | bytes 4194304 | tf_op jit(solution)/shard_map/all_to_all | solution.py:157
  22.8 1.3 dynamic-slice_bitcast_fusion.1
  24.1 1.9 %collective-permute-start.3 = (bf16[384,512]{1,0:T(8,128)(2,1)S(1)}, bf16[384,512]{1,0:T(8,128)(2,1)S(1)}, u32[]{:S(2)}, u32[]{:S(2)}) collective-permute-start(bf16[384,512]{1,0:T(8,128)(2,1)S(1)} %get-tuple-element.6), channel_id=1, source_target_pairs={{0,1},{1,2},{2,3},{3,0},{4,5},{5,6},{6,7},{7,4},{8,9},{9,10},{10,1... | collective-permute-start | bytes 1179656 | tf_op jit(solution)/shard_map/ppermute | solution.py:14
  26.0 8.2 %collective-permute-start.4 = (bf16[384,512]{1,0:T(8,128)(2,1)S(1)}, bf16[384,512]{1,0:T(8,128)(2,1)S(1)}, u32[]{:S(2)}, u32[]{:S(2)}) collective-permute-start(bf16[384,512]{1,0:T(8,128)(2,1)S(1)} %get-tuple-element.7), channel_id=1, source_target_pairs={{0,2},{1,3},{2,0},{3,1},{4,6},{5,7},{6,4},{7,5},{8,10},{9,11},{10,... | collective-permute-start | bytes 1179656 | tf_op jit(solution)/shard_map/ppermute | solution.py:14
  34.2 1.9 %collective-permute-start.5 = (bf16[384,512]{1,0:T(8,128)(2,1)S(1)}, bf16[384,512]{1,0:T(8,128)(2,1)S(1)}, u32[]{:S(2)}, u32[]{:S(2)}) collective-permute-start(bf16[384,512]{1,0:T(8,128)(2,1)S(1)} %get-tuple-element.5), channel_id=1, source_target_pairs={{0,3},{1,0},{2,1},{3,2},{4,7},{5,4},{6,5},{7,6},{8,11},{9,8},{10,9... | collective-permute-start | bytes 1179656 | tf_op jit(solution)/shard_map/ppermute | solution.py:14
  36.1 3.6 %collective-permute-done.3.refs_5_ = bf16[384,512]{1,0:T(8,128)(2,1)S(1)} collective-permute-done((bf16[384,512]{1,0:T(8,128)(2,1)S(1)}, bf16[384,512]{1,0:T(8,128)(2,1)S(1)}, u32[]{:S(2)}, u32[]{:S(2)}) %collective-permute-start.3) | collective-permute-done | bytes 393248 | tf_op jit(solution)/shard_map/ppermute | solution.py:14
  39.7 13.7 %collective-permute-done.4.refs_6_ = bf16[384,512]{1,0:T(8,128)(2,1)S(1)} collective-permute-done((bf16[384,512]{1,0:T(8,128)(2,1)S(1)}, bf16[384,512]{1,0:T(8,128)(2,1)S(1)}, u32[]{:S(2)}, u32[]{:S(2)}) %collective-permute-start.4) | collective-permute-done | bytes 393248 | tf_op jit(solution)/shard_map/ppermute | solution.py:14
  53.5 17.7 %collective-permute-done.5.refs_7_ = bf16[384,512]{1,0:T(8,128)(2,1)S(1)} collective-permute-done((bf16[384,512]{1,0:T(8,128)(2,1)S(1)}, bf16[384,512]{1,0:T(8,128)(2,1)S(1)}, u32[]{:S(2)}, u32[]{:S(2)}) %collective-permute-start.5) | collective-permute-done | bytes 393248 | tf_op jit(solution)/shard_map/ppermute | solution.py:14
  71.2 1.1 fusion.4
  72.3 3.2 %collective-permute-start.6 = (bf16[1152,256]{1,0:T(8,128)(2,1)}, bf16[1152,256]{1,0:T(8,128)(2,1)S(1)}, u32[]{:S(2)}, u32[]{:S(2)}) collective-permute-start(bf16[1152,256]{1,0:T(8,128)(2,1)} %get-tuple-element.9), channel_id=1, source_target_pairs={{0,128},{64,192},{128,256},{192,320},{256,384},{320,448},{384,512}... | collective-permute-start | bytes 1769480 | tf_op jit(solution)/shard_map/ppermute | solution.py:14
  75.5 4.5 %collective-permute-start.7 = (bf16[1152,256]{1,0:T(8,128)(2,1)}, bf16[1152,256]{1,0:T(8,128)(2,1)S(1)}, u32[]{:S(2)}, u32[]{:S(2)}) collective-permute-start(bf16[1152,256]{1,0:T(8,128)(2,1)} %get-tuple-element.8), channel_id=1, source_target_pairs={{0,896},{64,960},{128,0},{192,64},{256,128},{320,192},{384,256},{4... | collective-permute-start | bytes 1769480 | tf_op jit(solution)/shard_map/ppermute | solution.py:14
  80.0 0.0 all-to-all-done
  80.0 5.7 %shard_map.64.refs_0_ = bf16[256,384]{1,0:T(8,128)(2,1)} custom-call(bf16[256,4096]{1,0:T(8,128)(2,1)} %bitcast.1.x_ref, bf16[4096,384]{1,0:T(8,128)(2,1)} %bitcast.18, bf16[4096,384]{1,0:T(8,128)(2,1)} %bitcast.19), custom_call_target="tpu_custom_call" | custom-call | flops 1610612736 | bytes 8585216 | tf_op jit(solution)/shard_map/pallas_call | solution.py:53
  85.6 0.0 copy-start.1
  85.6 2.3 %collective-permute-start = (bf16[256,384]{1,0:T(8,128)(2,1)}, bf16[256,384]{1,0:T(8,128)(2,1)S(1)}, u32[]{:S(2)}, u32[]{:S(2)}) collective-permute-start(bf16[256,384]{1,0:T(8,128)(2,1)} %shard_map.64.refs_0_), channel_id=1, source_target_pairs={{0,1},{1,2},{2,3},{3,0},{4,5},{5,6},{6,7},{7,4},{8,9},{9,10},{10,1... | collective-permute-start | bytes 589832 | tf_op jit(solution)/shard_map/ppermute | solution.py:14
  87.9 7.1 %collective-permute-start.1 = (bf16[256,384]{1,0:T(8,128)(2,1)}, bf16[256,384]{1,0:T(8,128)(2,1)S(1)}, u32[]{:S(2)}, u32[]{:S(2)}) collective-permute-start(bf16[256,384]{1,0:T(8,128)(2,1)} %shard_map.64.refs_0_), channel_id=1, source_target_pairs={{0,2},{1,3},{2,0},{3,1},{4,6},{5,7},{6,4},{7,5},{8,10},{9,11},{10,... | collective-permute-start | bytes 589832 | tf_op jit(solution)/shard_map/ppermute | solution.py:14
  95.0 1.9 %collective-permute-start.2 = (bf16[256,384]{1,0:T(8,128)(2,1)}, bf16[256,384]{1,0:T(8,128)(2,1)}, u32[]{:S(2)}, u32[]{:S(2)}) collective-permute-start(bf16[256,384]{1,0:T(8,128)(2,1)} %shard_map.64.refs_0_), channel_id=1, source_target_pairs={{0,3},{1,0},{2,1},{3,2},{4,7},{5,4},{6,5},{7,6},{8,11},{9,8},{10,9... | collective-permute-start | bytes 589832 | tf_op jit(solution)/shard_map/ppermute | solution.py:14
  96.9 1.2 dynamic-slice_bitcast_fusion.refs_4_
  98.1 0.0 copy-start.2
  98.1 0.0 collective-permute-done.6.refs_8_
  98.1 0.0 collective-permute-done.7.refs_9_
  98.2 0.0 collective-permute-done.refs_1_
  98.2 7.8 %collective-permute-done.1.refs_2_ = bf16[256,384]{1,0:T(8,128)(2,1)S(1)} collective-permute-done((bf16[256,384]{1,0:T(8,128)(2,1)}, bf16[256,384]{1,0:T(8,128)(2,1)S(1)}, u32[]{:S(2)}, u32[]{:S(2)}) %collective-permute-start.1) | collective-permute-done | bytes 196640 | tf_op jit(solution)/shard_map/ppermute | solution.py:14
  106.0 0.4 collective-permute-done.2.refs_3_
  106.4 0.0 copy-done.1
  106.4 3.0 %shard_map.65 = bf16[256,1024]{1,0:T(8,128)(2,1)} custom-call(bf16[256,384]{1,0:T(8,128)(2,1)S(1)} %copy-done.1, bf16[256,384]{1,0:T(8,128)(2,1)S(1)} %collective-permute-done.refs_1_, bf16[256,384]{1,0:T(8,128)(2,1)S(1)} %collective-permute-done.1.refs_2_, bf16[256,384]{1,0:T(8,128)(2,1)} %collective-permute-done.2.refs_3_, ...), custom_call_target="tpu_custom_call" | custom-call | flops 805306368 | bytes 4456448 | tf_op jit(solution)/shard_map/pallas_call | solution.py:103
  109.3 9.3 %all-to-all-start.1 = ((bf16[16,16,1024]{2,1,0:T(8,128)(2,1)}), bf16[16,16,1024]{2,1,0:T(8,128)(2,1)S(1)}, u32[]{:S(2)}, u32[]{:S(2)}) async-start(bf16[16,16,1024]{2,1,0:T(8,128)(2,1)} %bitcast.8), calls=%async_computation.1 | async-start | bytes 1048576 | tf_op jit(solution)/shard_map/all_to_all | solution.py:164
  118.7 0.0 copy-done.2
  118.7 0.1 fusion.2
  118.8 17.1 %all-to-all-done.1 = bf16[16,16,1024]{2,1,0:T(8,128)(2,1)S(1)} async-done(((bf16[16,16,1024]{2,1,0:T(8,128)(2,1)}), bf16[16,16,1024]{2,1,0:T(8,128)(2,1)S(1)}, u32[]{:S(2)}, u32[]{:S(2)}) %all-to-all-start.1) | async-done | bytes 524320 | tf_op jit(solution)/shard_map/all_to_all | solution.py:164
  135.9 0.9 convolution_convert_fusion.1
  (3 shorter events, 0.1 us)
Async XLA Ops:
  0.0 2.4 %copy-start = (bf16[64,4096]{1,0:T(8,128)(2,1)S(1)}, bf16[64,4096]{1,0:T(8,128)(2,1)}, u32[]{:S(2)}) copy-start(bf16[64,4096]{1,0:T(8,128)(2,1)} %param.6) | copy-start | bytes 1572868
  4.5 75.5 %all-to-all-start = ((bf16[16,16,4096]{2,1,0:T(8,128)(2,1)}), bf16[16,16,4096]{2,1,0:T(8,128)(2,1)}, u32[]{:S(2)}, u32[]{:S(2)}) async-start(bf16[16,16,4096]{2,1,0:T(8,128)(2,1)} %bitcast), calls=%async_computation | async-start | bytes 4194304 | tf_op jit(solution)/shard_map/all_to_all | solution.py:157
  24.1 15.6 %collective-permute-start.3 = (bf16[384,512]{1,0:T(8,128)(2,1)S(1)}, bf16[384,512]{1,0:T(8,128)(2,1)S(1)}, u32[]{:S(2)}, u32[]{:S(2)}) collective-permute-start(bf16[384,512]{1,0:T(8,128)(2,1)S(1)} %get-tuple-element.6), channel_id=1, source_target_pairs={{0,1},{1,2},{2,3},{3,0},{4,5},{5,6},{6,7},{7,4},{8,9},{9,10},{10,1... | collective-permute-start | bytes 1179656 | tf_op jit(solution)/shard_map/ppermute | solution.py:14
  26.0 27.4 %collective-permute-start.4 = (bf16[384,512]{1,0:T(8,128)(2,1)S(1)}, bf16[384,512]{1,0:T(8,128)(2,1)S(1)}, u32[]{:S(2)}, u32[]{:S(2)}) collective-permute-start(bf16[384,512]{1,0:T(8,128)(2,1)S(1)} %get-tuple-element.7), channel_id=1, source_target_pairs={{0,2},{1,3},{2,0},{3,1},{4,6},{5,7},{6,4},{7,5},{8,10},{9,11},{10,... | collective-permute-start | bytes 1179656 | tf_op jit(solution)/shard_map/ppermute | solution.py:14
  34.2 36.9 %collective-permute-start.5 = (bf16[384,512]{1,0:T(8,128)(2,1)S(1)}, bf16[384,512]{1,0:T(8,128)(2,1)S(1)}, u32[]{:S(2)}, u32[]{:S(2)}) collective-permute-start(bf16[384,512]{1,0:T(8,128)(2,1)S(1)} %get-tuple-element.5), channel_id=1, source_target_pairs={{0,3},{1,0},{2,1},{3,2},{4,7},{5,4},{6,5},{7,6},{8,11},{9,8},{10,9... | collective-permute-start | bytes 1179656 | tf_op jit(solution)/shard_map/ppermute | solution.py:14
  72.3 25.9 %collective-permute-start.6 = (bf16[1152,256]{1,0:T(8,128)(2,1)}, bf16[1152,256]{1,0:T(8,128)(2,1)S(1)}, u32[]{:S(2)}, u32[]{:S(2)}) collective-permute-start(bf16[1152,256]{1,0:T(8,128)(2,1)} %get-tuple-element.9), channel_id=1, source_target_pairs={{0,128},{64,192},{128,256},{192,320},{256,384},{320,448},{384,512}... | collective-permute-start | bytes 1769480 | tf_op jit(solution)/shard_map/ppermute | solution.py:14
  75.5 22.7 %collective-permute-start.7 = (bf16[1152,256]{1,0:T(8,128)(2,1)}, bf16[1152,256]{1,0:T(8,128)(2,1)S(1)}, u32[]{:S(2)}, u32[]{:S(2)}) collective-permute-start(bf16[1152,256]{1,0:T(8,128)(2,1)} %get-tuple-element.8), channel_id=1, source_target_pairs={{0,896},{64,960},{128,0},{192,64},{256,128},{320,192},{384,256},{4... | collective-permute-start | bytes 1769480 | tf_op jit(solution)/shard_map/ppermute | solution.py:14
  85.6 20.7 %copy-start.1 = (bf16[256,384]{1,0:T(8,128)(2,1)S(1)}, bf16[256,384]{1,0:T(8,128)(2,1)}, u32[]{:S(2)}) copy-start(bf16[256,384]{1,0:T(8,128)(2,1)} %shard_map.64.refs_0_) | copy-start | bytes 589828
  85.6 12.5 %collective-permute-start = (bf16[256,384]{1,0:T(8,128)(2,1)}, bf16[256,384]{1,0:T(8,128)(2,1)S(1)}, u32[]{:S(2)}, u32[]{:S(2)}) collective-permute-start(bf16[256,384]{1,0:T(8,128)(2,1)} %shard_map.64.refs_0_), channel_id=1, source_target_pairs={{0,1},{1,2},{2,3},{3,0},{4,5},{5,6},{6,7},{7,4},{8,9},{9,10},{10,1... | collective-permute-start | bytes 589832 | tf_op jit(solution)/shard_map/ppermute | solution.py:14
  87.9 18.1 %collective-permute-start.1 = (bf16[256,384]{1,0:T(8,128)(2,1)}, bf16[256,384]{1,0:T(8,128)(2,1)S(1)}, u32[]{:S(2)}, u32[]{:S(2)}) collective-permute-start(bf16[256,384]{1,0:T(8,128)(2,1)} %shard_map.64.refs_0_), channel_id=1, source_target_pairs={{0,2},{1,3},{2,0},{3,1},{4,6},{5,7},{6,4},{7,5},{8,10},{9,11},{10,... | collective-permute-start | bytes 589832 | tf_op jit(solution)/shard_map/ppermute | solution.py:14
  95.0 11.4 %collective-permute-start.2 = (bf16[256,384]{1,0:T(8,128)(2,1)}, bf16[256,384]{1,0:T(8,128)(2,1)}, u32[]{:S(2)}, u32[]{:S(2)}) collective-permute-start(bf16[256,384]{1,0:T(8,128)(2,1)} %shard_map.64.refs_0_), channel_id=1, source_target_pairs={{0,3},{1,0},{2,1},{3,2},{4,7},{5,4},{6,5},{7,6},{8,11},{9,8},{10,9... | collective-permute-start | bytes 589832 | tf_op jit(solution)/shard_map/ppermute | solution.py:14
  98.1 20.6 %copy-start.2 = (bf16[64,2]{0,1:T(2,128)(2,1)S(1)}, bf16[64,2]{0,1:T(2,128)(2,1)}, u32[]{:S(2)}) copy-start(bf16[64,2]{0,1:T(2,128)(2,1)} %param.8) | copy-start | bytes 772
  109.3 26.6 %all-to-all-start.1 = ((bf16[16,16,1024]{2,1,0:T(8,128)(2,1)}), bf16[16,16,1024]{2,1,0:T(8,128)(2,1)S(1)}, u32[]{:S(2)}, u32[]{:S(2)}) async-start(bf16[16,16,1024]{2,1,0:T(8,128)(2,1)} %bitcast.8), calls=%async_computation.1 | async-start | bytes 1048576 | tf_op jit(solution)/shard_map/all_to_all | solution.py:164

commit v3 on v0

v3 whole, which is shorter than its diff:
```python
import jax
import jax.numpy as jnp
from jax import lax
from jax.experimental import pallas as pl
from jax.experimental.pallas import tpu as pltpu
from jax.sharding import PartitionSpec as P


STEPS = 4
BF16, F32 = jnp.bfloat16, jnp.float32
IN_VMEM = pl.BlockSpec(memory_space=pltpu.VMEM)
IN_HBM = pl.BlockSpec(memory_space=pltpu.HBM)


def shift(x, axis, by):
    count = lax.axis_size(axis)
    return lax.ppermute(x, axis, [(i, (i + by) % count) for i in range(count)])


def dispatch_kernel(ids_ref, weights_ref, tokens_ref, out_ref, combine_ref, chosen):
    experts, capacity = combine_ref.shape[0], combine_ref.shape[1]
    routes, rows = ids_ref.shape

    @pl.when(pl.program_id(0) == 0)
    def _():
        expert = lax.broadcasted_iota(jnp.int32, (experts, rows), 0)
        named = jnp.zeros((experts, rows), F32)
        weight = jnp.zeros((experts, rows), F32)
        for k in range(routes):
            hit = ids_ref[k : k + 1, :] == expert
            named = jnp.where(hit, 1.0, named)
            weight = jnp.where(hit, weights_ref[k : k + 1, :].astype(F32), weight)
        earlier = lax.broadcasted_iota(jnp.int32, (rows, rows), 0) < lax.broadcasted_iota(
            jnp.int32, (rows, rows), 1
        )
        slot = jnp.dot(
            named.astype(BF16), jnp.where(earlier, 1.0, 0.0).astype(BF16), preferred_element_type=F32
        ).astype(jnp.int32)
        slot = jnp.where(named > 0.0, slot, -1)
        place = lax.broadcasted_iota(jnp.int32, (experts, capacity, rows), 1)
        taken = slot[:, None, :] == place
        chosen[...] = jnp.where(taken, 1.0, 0.0).reshape(experts * capacity, rows).astype(BF16)
        combine_ref[...] = jnp.where(taken, weight[:, None, :], 0.0).astype(BF16)

    out_ref[...] = jnp.dot(chosen[...], tokens_ref[...], preferred_element_type=F32).astype(BF16)


def dispatch_rows(expert_ids, route_weights, tokens, experts, capacity):
    rows, width = tokens.shape
    routes = expert_ids.shape[1]
    small = pl.BlockSpec((routes, rows), lambda i: (0, 0))
    return pl.pallas_call(
        dispatch_kernel,
        grid=(STEPS,),
        out_shape=(
            jax.ShapeDtypeStruct((experts * capacity, width), BF16),
            jax.ShapeDtypeStruct((experts, capacity, rows), BF16),
        ),
        in_specs=[small, small, pl.BlockSpec((rows, width // STEPS), lambda i: (0, i))],
        out_specs=(
            pl.BlockSpec((experts * capacity, width // STEPS), lambda i: (0, i)),
            pl.BlockSpec((experts, capacity, rows), lambda i: (0, 0, 0)),
        ),
        scratch_shapes=[pltpu.VMEM((experts * capacity, rows), BF16)],
        compiler_params=pltpu.CompilerParams(vmem_limit_bytes=60 * 2**20),
        cost_estimate=pl.CostEstimate(
            flops=2 * experts * capacity * rows * width,
            bytes_accessed=2 * (experts * capacity + rows) * width,
            transcendentals=0,
        ),
    )(expert_ids.T, route_weights.T, tokens)


def hidden_kernel(x_ref, gate_ref, up_ref, out_ref, x_buf, weights, sems):
    rows, width = x_ref.shape
    units = gate_ref.shape[1]
    depth = width // STEPS
    copies = []
    for k in range(STEPS):
        part = pl.ds(k * depth, depth)
        copies.append(
            (
                pltpu.make_async_copy(x_ref.at[:, part], x_buf.at[:, part], sems.at[0, k]),
                pltpu.make_async_copy(
                    gate_ref.at[part], weights.at[part, pl.ds(0, units)], sems.at[1, k]
                ),
                pltpu.make_async_copy(
                    up_ref.at[part], weights.at[part, pl.ds(units, units)], sems.at[2, k]
                ),
            )
        )
    for group in copies:
        for copy in group:
            copy.start()
    total = jnp.zeros((rows, 2 * units), F32)
    for k in range(STEPS):
        for copy in copies[k]:
            copy.wait()
        part = pl.ds(k * depth, depth)
        total += jnp.dot(x_buf[:, part], weights[part, :], preferred_element_type=F32)
    gate, up = total[:, :units], total[:, units:]
    out_ref[...] = (gate / (1.0 + jnp.exp(-gate)) * up).astype(out_ref.dtype)


def hidden_units(arrived, w_gate, w_up):
    rows, width = arrived.shape
    units = w_gate.shape[1]
    return pl.pallas_call(
        hidden_kernel,
        out_shape=jax.ShapeDtypeStruct((rows, units), BF16),
        in_specs=[IN_HBM] * 3,
        out_specs=IN_VMEM,
        scratch_shapes=[
            pltpu.VMEM((rows, width), BF16),
            pltpu.VMEM((width, 2 * units), BF16),
            pltpu.SemaphoreType.DMA((3, STEPS)),
        ],
        compiler_params=pltpu.CompilerParams(vmem_limit_bytes=56 * 2**20),
        cost_estimate=pl.CostEstimate(
            flops=4 * rows * width * units,
            bytes_accessed=2 * (rows * width + 2 * width * units + rows * units),
            transcendentals=rows * units,
        ),
    )(arrived, w_gate, w_up)


def down_kernel(mine, after, before, own_low, own_high, sent_low, sent_high, out_ref):
    sources, quarters, capacity, part = out_ref.shape
    pairs = ((after, own_low, sent_low), (before, own_high, sent_high))
    for side, (other, own, sent) in enumerate(pairs):
        for j in range(quarters // 2):
            cols = pl.ds(j * part, part)
            total = jnp.dot(mine[...], own[:, cols], preferred_element_type=F32)
            total += jnp.dot(other[...], sent[:, cols], preferred_element_type=F32)
            out_ref[:, side * (quarters // 2) + j] = total.astype(BF16).reshape(
                sources, capacity, part
            )


def project_down(operands, sources, quarters, capacity):
    rows, units = operands[0].shape
    width = operands[-1].shape[1]
    return pl.pallas_call(
        down_kernel,
        out_shape=jax.ShapeDtypeStruct((sources, quarters, capacity, 2 * width // quarters), BF16),
        in_specs=[IN_VMEM] * len(operands),
        out_specs=IN_VMEM,
        compiler_params=pltpu.CompilerParams(vmem_limit_bytes=24 * 2**20),
        cost_estimate=pl.CostEstimate(
            flops=8 * rows * units * width,
            bytes_accessed=2 * (3 * rows * units + 4 * units * width + 2 * rows * width),
            transcendentals=0,
        ),
    )(*operands)


def combine_kernel(maps_ref, rows_ref, out_ref):
    rows = maps_ref.shape[0] // 2
    half = rows_ref.shape[1]
    total = jnp.dot(maps_ref[...], rows_ref[...], preferred_element_type=F32).astype(BF16)
    out_ref[:, :half] = total[:rows]
    out_ref[:, half:] = total[rows:]


def combine_rows(maps, returned):
    rows, depth = maps.shape
    half = returned.shape[1]
    return pl.pallas_call(
        combine_kernel,
        out_shape=jax.ShapeDtypeStruct((rows // 2, 2 * half), BF16),
        in_specs=[IN_VMEM] * 2,
        out_specs=IN_VMEM,
        compiler_params=pltpu.CompilerParams(vmem_limit_bytes=24 * 2**20),
        cost_estimate=pl.CostEstimate(
            flops=2 * rows * depth * half,
            bytes_accessed=2 * (rows * depth + depth * half + rows * half),
            transcendentals=0,
        ),
    )(maps, returned)


def weight_columns(w_down, first, half, choice):
    units = w_down.shape[0]
    start = first + choice * half
    return jnp.concatenate(
        [lax.dynamic_slice(w_down, (0, start + k * 2 * half), (units, half)) for k in range(2)], axis=1
    )


def per_device(tokens, expert_ids, route_weights, w_gate, w_up, w_down):
    tok_rows, width = tokens.shape
    route_count = expert_ids.shape[1]
    sources = lax.axis_size("expert")
    quarters = lax.axis_size("etp")
    experts = sources
    capacity = 2 * tok_rows * route_count // experts
    quarter = width // quarters
    half = quarter // 2
    here = lax.axis_index("etp")
    odd = here % 2

    outgoing, combine = dispatch_rows(expert_ids, route_weights, tokens, experts, capacity)
    arrived = lax.all_to_all(
        outgoing.reshape(experts, capacity, width), "expert", split_axis=0, concat_axis=0, tiled=True
    )

    down = w_down[0]
    own_low = weight_columns(down, 0, half, odd)
    own_high = weight_columns(down, width // 2, half, 1 - odd)
    sent_low = shift(weight_columns(down, 0, half, 1 - odd), "etp", -1)
    sent_high = shift(weight_columns(down, width // 2, half, odd), "etp", 1)

    mine = hidden_units(arrived.reshape(sources * capacity, width), w_gate[0], w_up[0])
    after, before = shift(mine, "etp", -1), shift(mine, "etp", 1)
    expert_out = project_down(
        (mine, after, before, own_low, own_high, sent_low, sent_high), sources, quarters, capacity
    )
    returned = lax.all_to_all(
        expert_out.reshape(sources * quarters, capacity, half),
        ("expert", "etp"),
        split_axis=0,
        concat_axis=0,
        tiled=True,
    )
    first_half = (jnp.arange(quarters) % 2 == here // (quarters // 2))[None, None, :, None]
    weights = jnp.transpose(combine.reshape(experts * capacity, tok_rows))
    spread = jnp.broadcast_to(
        weights.reshape(tok_rows, experts, 1, capacity), (tok_rows, experts, quarters, capacity)
    )
    maps = jnp.stack([jnp.where(first_half, spread, 0), jnp.where(first_half, 0, spread)])
    return combine_rows(
        maps.reshape(2 * tok_rows, experts * quarters * capacity),
        returned.reshape(experts * quarters * capacity, half),
    )


def solution(mesh):
    return jax.shard_map(
        per_device,
        mesh=mesh,
        in_specs=(
            P(("dp", "expert"), None),
            P(("dp", "expert"), None),
            P(("dp", "expert"), None),
            P("expert", None, "etp"),
            P("expert", None, "etp"),
            P("expert", "etp", None),
        ),
        out_specs=P(("dp", "expert"), "etp"),
        check_vma=False,
    )
```

time: 171 us -> 138 us (0.81)
  blocking collectives: 125 us -> 0 us
  waiting for transfers between devices: 14.9 us -> 70.1 us
  starting transfers between devices: 4.13 us -> 47.9 us
  Pallas kernels: 0 us -> 12.9 us
  matrix products: 12.3 us -> 0 us
  local copies, waits for them, and re-layouts: 9.3 us -> 1.69 us
    all_to_all x2 -> x0, blocking collectives: 125 us -> none  [the longest x1 67.6 us: per_device(): lax.all_to_all(outgoing.reshape(experts, capacity, width), 'expert', spli...]
    all_to_all x1 -> x2, waiting for transfers between devices: 14.9 us -> 65.1 us  [the longest x1 37.9 us: per_device(): lax.all_to_all(outgoing.reshape(experts, capacity, width), 'expert', spli...]
    all_to_all x1 -> x2, starting transfers between devices: 4.13 us -> 31.9 us  [the longest x1 18.5 us: per_device(): lax.all_to_all(outgoing.reshape(experts, capacity, width), 'expert', spli...]
    ppermute x0 -> x4, starting transfers between devices: none -> 16 us  [shift(): return lax.ppermute(x, axis, [(i, (i + by) % count) for i in range(count)])]
    pallas_call x0 -> x4, Pallas kernels: none -> 12.9 us  [the longest x1 5.44 us: hidden_units(): pl.pallas_call(hidden_kernel, out_shape=jax.ShapeDtypeStruct((rows, units...]
    dot_general x4 -> x0, matrix products: 12.3 us -> none  [the longest x1 6.37 us: per_device(): jnp.einsum('sech,ehd->secd', hidden, w_down, preferred_element_type=jnp.f...]
    convert_element_type x2 -> x0, local copies, waits for them, and re-layouts: 6.73 us -> none  [per_device(): partial_out.astype(jnp.bfloat16)]
    ppermute x0 -> x4, waiting for transfers between devices: none -> 4.98 us  [shift(): return lax.ppermute(x, axis, [(i, (i + by) % count) for i in range(count)])]
  transfers between devices with their start and end apart: 1 -> 6, of which waited for: 1 -> 4; matrix products, arithmetic and copies ran while one was open for 0% -> 4% of each run, Pallas kernels for 0% -> 4%
where the time goes in v3:
time: 138 us; the launch traced here: 137 us
  waiting for transfers between devices  70.1 us (51%)
  starting transfers between devices  47.9 us (35%)
  Pallas kernels  12.9 us (9%)
  other arithmetic  4.4 us (3%)
  local copies, waits for them, and re-layouts  1.69 us (1%)
    all_to_all x1, waiting for transfers between devices, per_device(): lax.all_to_all(outgoing.reshape(experts, capacity, width), 'expert', spli...  37.9 us
    all_to_all x1, waiting for transfers between devices, per_device(): lax.all_to_all(expert_out.reshape(sources * quarters, capacity, half), ('...  27.2 us
    all_to_all x1, starting transfers between devices, per_device(): lax.all_to_all(outgoing.reshape(experts, capacity, width), 'expert', spli...  18.5 us
    ppermute x4, starting transfers between devices, shift(): return lax.ppermute(x, axis, [(i, (i + by) % count) for i in range(count)])  16 us
    all_to_all x1, starting transfers between devices, per_device(): lax.all_to_all(expert_out.reshape(sources * quarters, capacity, half), ('...  13.4 us
    pallas_call x1, Pallas kernels, hidden_units(): pl.pallas_call(hidden_kernel, out_shape=jax.ShapeDtypeStruct((rows, units...  5.44 us
    ppermute x4, waiting for transfers between devices, shift(): return lax.ppermute(x, axis, [(i, (i + by) % count) for i in range(count)])  4.98 us
    pallas_call x1, Pallas kernels, dispatch_rows(): pl.pallas_call(dispatch_kernel, grid=(STEPS,), out_shape=(jax.ShapeDtypeS...  4.23 us
  transfers between devices with their start and end apart: 6, of which 4 were waited for; matrix products, arithmetic and copies ran while one was open for 4% of the time, Pallas kernels for 4%

profile of v3, /device:TPU:1, one launch (start us, length us, event | category | flops | bytes accessed | tf_op | source)
XLA Modules:
  0.0 137.2 jit_solution(254677935481854095)
XLA Ops:
  0.0 4.2 %shard_map.64 = (bf16[256,4096]{1,0:T(8,128)(2,1)}, bf16[16,16,64]{2,1,0:T(8,128)(2,1)}) custom-call(s32[2,64]{1,0:T(2,128)} %bitcast.36, bf16[2,64]{1,0:T(2,128)(2,1)} %bitcast.37, bf16[64,4096]{1,0:T(8,128)(2,1)} %tokens_ref.1), custom_call_target="tpu_custom_call" | custom-call | flops 134217728 | bytes 2621440 | tf_op jit(solution)/shard_map/pallas_call | solution.py:52
  4.2 0.0 copy-start.1
  4.2 18.5 %all-to-all-start = ((bf16[16,16,4096]{2,1,0:T(8,128)(2,1)}), bf16[16,16,4096]{2,1,0:T(8,128)(2,1)}, u32[]{:S(2)}, u32[]{:S(2)}) async-start(bf16[16,16,4096]{2,1,0:T(8,128)(2,1)} %bitcast.34), calls=%async_computation | async-start | bytes 4194304 | tf_op jit(solution)/shard_map/all_to_all | solution.py:203
  22.8 0.0 copy-done.1
  22.8 1.3 dynamic-slice_bitcast_fusion.1
  24.1 1.0 pad_maximum_fusion.2
  25.0 6.1 %collective-permute-start.2 = (bf16[384,1024]{1,0:T(8,128)(2,1)}, bf16[384,1024]{1,0:T(8,128)(2,1)S(1)}, u32[]{:S(2)}, u32[]{:S(2)}) collective-permute-start(bf16[384,1024]{1,0:T(8,128)(2,1)} %pad_maximum_fusion.2), channel_id=1, source_target_pairs={{0,3},{1,0},{2,1},{3,2},{4,7},{5,4},{6,5},{7,6},{8,11},{9,8},{10,9... | collective-permute-start | bytes 2359304 | tf_op jit(solution)/shard_map/ppermute | solution.py:17
  31.1 1.0 pad_maximum_fusion.3
  32.2 1.9 %collective-permute-start.3 = (bf16[384,1024]{1,0:T(8,128)(2,1)}, bf16[384,1024]{1,0:T(8,128)(2,1)S(1)}, u32[]{:S(2)}, u32[]{:S(2)}) collective-permute-start(bf16[384,1024]{1,0:T(8,128)(2,1)} %pad_maximum_fusion.3), channel_id=1, source_target_pairs={{0,1},{1,2},{2,3},{3,0},{4,5},{5,6},{6,7},{7,4},{8,9},{9,10},{10,1... | collective-permute-start | bytes 2359304 | tf_op jit(solution)/shard_map/ppermute | solution.py:17
  34.1 37.9 %all-to-all-done = bf16[16,16,4096]{2,1,0:T(8,128)(2,1)} async-done(((bf16[16,16,4096]{2,1,0:T(8,128)(2,1)}), bf16[16,16,4096]{2,1,0:T(8,128)(2,1)}, u32[]{:S(2)}, u32[]{:S(2)}) %all-to-all-start) | async-done | bytes 2097184 | tf_op jit(solution)/shard_map/all_to_all | solution.py:203
  72.0 0.0 copy-start.2
  72.0 0.0 copy-start.3
  72.0 0.0 copy-start.4
  72.0 5.4 %shard_map.65.mine = bf16[256,384]{1,0:T(8,128)(2,1)} custom-call(bf16[256,4096]{1,0:T(8,128)(2,1)} %bitcast.6.x_ref, bf16[4096,384]{1,0:T(8,128)(2,1)} %bitcast.32, bf16[4096,384]{1,0:T(8,128)(2,1)} %bitcast.33), custom_call_target="tpu_custom_call" | custom-call | flops 1610612736 | bytes 8585216 | tf_op jit(solution)/shard_map/pallas_call | solution.py:108
  77.5 1.9 %collective-permute-start.1 = (bf16[256,384]{1,0:T(8,128)(2,1)}, bf16[256,384]{1,0:T(8,128)(2,1)S(1)}, u32[]{:S(2)}, u32[]{:S(2)}) collective-permute-start(bf16[256,384]{1,0:T(8,128)(2,1)} %shard_map.65.mine), channel_id=1, source_target_pairs={{0,1},{1,2},{2,3},{3,0},{4,5},{5,6},{6,7},{7,4},{8,9},{9,10},{10,1... | collective-permute-start | bytes 589832 | tf_op jit(solution)/shard_map/ppermute | solution.py:17
  79.4 6.0 %collective-permute-start = (bf16[256,384]{1,0:T(8,128)(2,1)}, bf16[256,384]{1,0:T(8,128)(2,1)S(1)}, u32[]{:S(2)}, u32[]{:S(2)}) collective-permute-start(bf16[256,384]{1,0:T(8,128)(2,1)} %shard_map.65.mine), channel_id=1, source_target_pairs={{0,3},{1,0},{2,1},{3,2},{4,7},{5,4},{6,5},{7,6},{8,11},{9,8},{10,9... | collective-permute-start | bytes 589832 | tf_op jit(solution)/shard_map/ppermute | solution.py:17
  85.4 0.0 copy-done.2
  85.4 0.0 copy-done.3
  85.5 0.0 copy-done.4
  85.5 0.0 copy-start
  85.5 0.2 pad_maximum_fusion
  85.7 0.0 collective-permute-done.2.sent_low
  85.7 0.0 collective-permute-done.3.sent_high
  85.7 3.1 %collective-permute-done.1.before = bf16[256,384]{1,0:T(8,128)(2,1)S(1)} collective-permute-done((bf16[256,384]{1,0:T(8,128)(2,1)}, bf16[256,384]{1,0:T(8,128)(2,1)S(1)}, u32[]{:S(2)}, u32[]{:S(2)}) %collective-permute-start.1) | collective-permute-done | bytes 196640 | tf_op jit(solution)/shard_map/ppermute | solution.py:17
  88.8 1.9 %collective-permute-done.after = bf16[256,384]{1,0:T(8,128)(2,1)S(1)} collective-permute-done((bf16[256,384]{1,0:T(8,128)(2,1)}, bf16[256,384]{1,0:T(8,128)(2,1)S(1)}, u32[]{:S(2)}, u32[]{:S(2)}) %collective-permute-start) | collective-permute-done | bytes 196640 | tf_op jit(solution)/shard_map/ppermute | solution.py:17
  90.7 0.0 copy-done
  90.7 2.2 %shard_map.66 = bf16[16,4,16,512]{3,2,1,0:T(8,128)(2,1)} custom-call(bf16[256,384]{1,0:T(8,128)(2,1)S(1)} %copy-done, bf16[256,384]{1,0:T(8,128)(2,1)S(1)} %collective-permute-done.after, bf16[256,384]{1,0:T(8,128)(2,1)S(1)} %collective-permute-done.1.before, bf16[384,1024]{1,0:T(8,128)(2,1)S(1)} %get-tuple-element.19.own_low, ...), custom_call_target="tpu_custom_call" | custom-call | flops 805306368 | bytes 4784128 | tf_op jit(solution)/shard_map/pallas_call | solution.py:143
  92.9 0.0 copy-start.5
  92.9 13.4 %all-to-all-start.1 = ((bf16[64,16,512]{2,1,0:T(8,128)(2,1)}), bf16[64,16,512]{2,1,0:T(8,128)(2,1)S(1)}, u32[]{:S(2)}, u32[]{:S(2)}) async-start(bf16[64,16,512]{2,1,0:T(8,128)(2,1)} %bitcast.17), calls=%async_computation.1 | async-start | bytes 2097152 | tf_op jit(solution)/shard_map/all_to_all | solution.py:218
  106.4 0.0 copy-done.5
  106.4 0.8 broadcast_select_fusion.1
  107.2 1.4 %pad_maximum_fusion.4 = bf16[2,64,16,4,16]{1,0,4,3,2:T(2,128)(2,1)S(1)} fusion(bf16[1,64,16,4,16]{1,0,4,3,2:T(2,128)(2,1)S(1)} %get-tuple-element.18, bf16[1,64,16,4,16]{1,0,4,3,2:T(2,128)(2,1)S(1)} %get-tuple-element.17), kind=kLoop, calls=%fused_computation.6 | loop fusion | flops 524288 | bytes 524288 | tf_op jit(solution)/shard_map/stack | solution.py:230
  108.6 0.2 reshape.45
  108.8 0.1 copy.8.maps_ref
  109.0 27.2 %all-to-all-done.1 = bf16[64,16,512]{2,1,0:T(8,128)(2,1)S(1)} async-done(((bf16[64,16,512]{2,1,0:T(8,128)(2,1)}), bf16[64,16,512]{2,1,0:T(8,128)(2,1)S(1)}, u32[]{:S(2)}, u32[]{:S(2)}) %all-to-all-start.1) | async-done | bytes 1048608 | tf_op jit(solution)/shard_map/all_to_all | solution.py:218
  136.2 1.0 shard_map.67
  (1 shorter events, 0.0 us)
Async XLA Ops:
  4.2 18.5 %copy-start.1 = (bf16[1,384,4096]{2,1,0:T(8,128)(2,1)S(1)}, bf16[1,384,4096]{2,1,0:T(8,128)(2,1)}, u32[]{:S(2)}) copy-start(bf16[1,384,4096]{2,1,0:T(8,128)(2,1)} %param.11) | copy-start | bytes 9437188
  4.2 67.8 %all-to-all-start = ((bf16[16,16,4096]{2,1,0:T(8,128)(2,1)}), bf16[16,16,4096]{2,1,0:T(8,128)(2,1)}, u32[]{:S(2)}, u32[]{:S(2)}) async-start(bf16[16,16,4096]{2,1,0:T(8,128)(2,1)} %bitcast.34), calls=%async_computation | async-start | bytes 4194304 | tf_op jit(solution)/shard_map/all_to_all | solution.py:203
  25.0 60.7 %collective-permute-start.2 = (bf16[384,1024]{1,0:T(8,128)(2,1)}, bf16[384,1024]{1,0:T(8,128)(2,1)S(1)}, u32[]{:S(2)}, u32[]{:S(2)}) collective-permute-start(bf16[384,1024]{1,0:T(8,128)(2,1)} %pad_maximum_fusion.2), channel_id=1, source_target_pairs={{0,3},{1,0},{2,1},{3,2},{4,7},{5,4},{6,5},{7,6},{8,11},{9,8},{10,9... | collective-permute-start | bytes 2359304 | tf_op jit(solution)/shard_map/ppermute | solution.py:17
  32.2 53.6 %collective-permute-start.3 = (bf16[384,1024]{1,0:T(8,128)(2,1)}, bf16[384,1024]{1,0:T(8,128)(2,1)S(1)}, u32[]{:S(2)}, u32[]{:S(2)}) collective-permute-start(bf16[384,1024]{1,0:T(8,128)(2,1)} %pad_maximum_fusion.3), channel_id=1, source_target_pairs={{0,1},{1,2},{2,3},{3,0},{4,5},{5,6},{6,7},{7,4},{8,9},{9,10},{10,1... | collective-permute-start | bytes 2359304 | tf_op jit(solution)/shard_map/ppermute | solution.py:17
  72.0 13.4 %copy-start.2 = (bf16[384,512]{1,0:T(8,128)(2,1)S(1)}, bf16[384,512]{1,0:T(8,128)(2,1)}, u32[]{:S(2)}) copy-start(bf16[384,512]{1,0:T(8,128)(2,1)} %get-tuple-element.13) | copy-start | bytes 1179652
  72.0 13.4 %copy-start.3 = (bf16[384,512]{1,0:T(8,128)(2,1)S(1)}, bf16[384,512]{1,0:T(8,128)(2,1)}, u32[]{:S(2)}) copy-start(bf16[384,512]{1,0:T(8,128)(2,1)} %get-tuple-element.14) | copy-start | bytes 1179652
  72.0 13.5 %copy-start.4 = (bf16[384,512]{1,0:T(8,128)(2,1)S(1)}, bf16[384,512]{1,0:T(8,128)(2,1)}, u32[]{:S(2)}) copy-start(bf16[384,512]{1,0:T(8,128)(2,1)} %get-tuple-element.15) | copy-start | bytes 1179652
  77.5 11.4 %collective-permute-start.1 = (bf16[256,384]{1,0:T(8,128)(2,1)}, bf16[256,384]{1,0:T(8,128)(2,1)S(1)}, u32[]{:S(2)}, u32[]{:S(2)}) collective-permute-start(bf16[256,384]{1,0:T(8,128)(2,1)} %shard_map.65.mine), channel_id=1, source_target_pairs={{0,1},{1,2},{2,3},{3,0},{4,5},{5,6},{6,7},{7,4},{8,9},{9,10},{10,1... | collective-permute-start | bytes 589832 | tf_op jit(solution)/shard_map/ppermute | solution.py:17
  79.4 11.3 %collective-permute-start = (bf16[256,384]{1,0:T(8,128)(2,1)}, bf16[256,384]{1,0:T(8,128)(2,1)S(1)}, u32[]{:S(2)}, u32[]{:S(2)}) collective-permute-start(bf16[256,384]{1,0:T(8,128)(2,1)} %shard_map.65.mine), channel_id=1, source_target_pairs={{0,3},{1,0},{2,1},{3,2},{4,7},{5,4},{6,5},{7,6},{8,11},{9,8},{10,9... | collective-permute-start | bytes 589832 | tf_op jit(solution)/shard_map/ppermute | solution.py:17
  85.5 5.2 %copy-start = (bf16[256,384]{1,0:T(8,128)(2,1)S(1)}, bf16[256,384]{1,0:T(8,128)(2,1)}, u32[]{:S(2)}) copy-start(bf16[256,384]{1,0:T(8,128)(2,1)} %shard_map.65.mine) | copy-start | bytes 589828
  92.9 13.4 %copy-start.5 = (bf16[16,16,64]{2,1,0:T(8,128)(2,1)S(1)}, bf16[16,16,64]{2,1,0:T(8,128)(2,1)}, u32[]{:S(2)}) copy-start(bf16[16,16,64]{2,1,0:T(8,128)(2,1)} %get-tuple-element.7) | copy-start | bytes 98308
  92.9 43.2 %all-to-all-start.1 = ((bf16[64,16,512]{2,1,0:T(8,128)(2,1)}), bf16[64,16,512]{2,1,0:T(8,128)(2,1)S(1)}, u32[]{:S(2)}, u32[]{:S(2)}) async-start(bf16[64,16,512]{2,1,0:T(8,128)(2,1)} %bitcast.17), calls=%async_computation.1 | async-start | bytes 2097152 | tf_op jit(solution)/shard_map/all_to_all | solution.py:218

commit v4 on v3

v4 whole, which is shorter than its diff:
```python
import jax
import jax.numpy as jnp
from jax import lax
from jax.experimental import pallas as pl
from jax.experimental.pallas import tpu as pltpu
from jax.sharding import PartitionSpec as P


STEPS = 2
PIECES = 4
DP_STEP = 2
SHARERS = 4
BF16, F32 = jnp.bfloat16, jnp.float32
IN_VMEM = pl.BlockSpec(memory_space=pltpu.VMEM)
IN_HBM = pl.BlockSpec(memory_space=pltpu.HBM)


def shift(x, axis, by):
    count = lax.axis_size(axis)
    return lax.ppermute(x, axis, [(i, (i + by) % count) for i in range(count)])


def dispatch_kernel(ids_ref, weights_ref, tokens_ref, out_ref, combine_ref, chosen):
    experts, capacity = combine_ref.shape[0], combine_ref.shape[1]
    routes, rows = ids_ref.shape

    @pl.when(pl.program_id(0) == 0)
    def _():
        expert = lax.broadcasted_iota(jnp.int32, (experts, rows), 0)
        named = jnp.zeros((experts, rows), F32)
        weight = jnp.zeros((experts, rows), F32)
        for k in range(routes):
            hit = ids_ref[k : k + 1, :] == expert
            named = jnp.where(hit, 1.0, named)
            weight = jnp.where(hit, weights_ref[k : k + 1, :].astype(F32), weight)
        earlier = lax.broadcasted_iota(jnp.int32, (rows, rows), 0) < lax.broadcasted_iota(
            jnp.int32, (rows, rows), 1
        )
        slot = jnp.dot(
            named.astype(BF16), jnp.where(earlier, 1.0, 0.0).astype(BF16), preferred_element_type=F32
        ).astype(jnp.int32)
        slot = jnp.where(named > 0.0, slot, -1)
        place = lax.broadcasted_iota(jnp.int32, (experts, capacity, rows), 1)
        taken = slot[:, None, :] == place
        chosen[...] = jnp.where(taken, 1.0, 0.0).reshape(experts * capacity, rows).astype(BF16)
        combine_ref[...] = jnp.where(taken, weight[:, None, :], 0.0).astype(BF16)

    out_ref[...] = jnp.dot(chosen[...], tokens_ref[...], preferred_element_type=F32).astype(BF16)


def dispatch_rows(expert_ids, route_weights, tokens, experts, capacity):
    rows, width = tokens.shape
    routes = expert_ids.shape[1]
    small = pl.BlockSpec((routes, rows), lambda i: (0, 0))
    return pl.pallas_call(
        dispatch_kernel,
        grid=(STEPS,),
        out_shape=(
            jax.ShapeDtypeStruct((experts * capacity, width), BF16),
            jax.ShapeDtypeStruct((experts, capacity, rows), BF16),
        ),
        in_specs=[small, small, pl.BlockSpec((rows, width // STEPS), lambda i: (0, i))],
        out_specs=(
            pl.BlockSpec((experts * capacity, width // STEPS), lambda i: (0, i)),
            pl.BlockSpec((experts, capacity, rows), lambda i: (0, 0, 0)),
        ),
        scratch_shapes=[pltpu.VMEM((experts * capacity, rows), BF16)],
        compiler_params=pltpu.CompilerParams(vmem_limit_bytes=60 * 2**20),
        cost_estimate=pl.CostEstimate(
            flops=2 * experts * capacity * rows * width,
            bytes_accessed=2 * (experts * capacity + rows) * width,
            transcendentals=0,
        ),
    )(expert_ids.T, route_weights.T, tokens)


def hidden_kernel(x_ref, gate_ref, up_ref, out_ref, x_buf, weights, sems):
    rows, width = x_ref.shape
    units = gate_ref.shape[1]
    depth = width // PIECES
    copies = []
    for k in range(PIECES):
        part = pl.ds(k * depth, depth)
        copies.append(
            (
                pltpu.make_async_copy(x_ref.at[:, part], x_buf.at[:, part], sems.at[2, k]),
                pltpu.make_async_copy(
                    gate_ref.at[part], weights.at[part, pl.ds(0, units)], sems.at[0, k]
                ),
                pltpu.make_async_copy(
                    up_ref.at[part], weights.at[part, pl.ds(units, units)], sems.at[1, k]
                ),
            )
        )
    for group in copies:
        for copy in group:
            copy.start()
    total = jnp.zeros((rows, 2 * units), F32)
    for k in range(PIECES):
        for copy in copies[k]:
            copy.wait()
        part = pl.ds(k * depth, depth)
        total += jnp.dot(x_buf[:, part], weights[part, :], preferred_element_type=F32)
    gate, up = total[:, :units], total[:, units:]
    out_ref[...] = (gate / (1.0 + jnp.exp(-gate)) * up).astype(out_ref.dtype)


def hidden_units(arrived, w_gate, w_up):
    rows, width = arrived.shape
    units = w_gate.shape[1]
    return pl.pallas_call(
        hidden_kernel,
        out_shape=pltpu.VMEM((rows, units), BF16),
        in_specs=[IN_HBM] * 3,
        out_specs=IN_VMEM,
        scratch_shapes=[
            pltpu.VMEM((rows, width), BF16),
            pltpu.VMEM((width, 2 * units), BF16),
            pltpu.SemaphoreType.DMA((3, PIECES)),
        ],
        compiler_params=pltpu.CompilerParams(vmem_limit_bytes=56 * 2**20),
        cost_estimate=pl.CostEstimate(
            flops=4 * rows * width * units,
            bytes_accessed=2 * (rows * width + 2 * width * units + rows * units),
            transcendentals=rows * units,
        ),
    )(arrived, w_gate, w_up)


def down_kernel(mine, other1, other2, other3, own, fetched, left, right, low, high, out_ref):
    piece, side = fetched.shape[1], low.shape[1]
    here = lax.rem(lax.div(lax.axis_index("dp"), DP_STEP), SHARERS)
    others = jnp.concatenate([other1[...], other2[...], other3[...]], axis=1)

    def project(start, block):
        columns = pl.ds(pl.multiple_of(start, side), block.shape[1])
        total = jnp.dot(mine[...], own[:, columns], preferred_element_type=F32)
        total += jnp.dot(others, block[...], preferred_element_type=F32)
        out_ref[:, columns] = total.astype(out_ref.dtype)

    project(here * piece, fetched)
    project(lax.rem(here + SHARERS - 1, SHARERS) * piece, left)
    project(lax.rem(here + 1, SHARERS) * piece, right)
    far = lax.rem(here + 2, SHARERS) * piece
    project(far, low)
    project(far + side, high)


def project_down(operands):
    rows, units = operands[0].shape
    own = operands[4]
    quarter = own.shape[1]
    return pl.pallas_call(
        down_kernel,
        out_shape=jax.ShapeDtypeStruct((rows, quarter), BF16),
        in_specs=[IN_VMEM] * len(operands),
        out_specs=IN_VMEM,
        compiler_params=pltpu.CompilerParams(vmem_limit_bytes=16 * 2**20),
        cost_estimate=pl.CostEstimate(
            flops=8 * rows * units * quarter,
            bytes_accessed=8 * (rows * units + units * quarter) + 2 * rows * quarter,
            transcendentals=0,
        ),
    )(*operands)


def down_weights(w_down, quarter, quarters):
    here = lax.axis_index("etp")
    units, piece = w_down.shape[0], quarter // SHARERS
    block = (lax.axis_index("dp") // DP_STEP) % SHARERS
    own = lax.dynamic_slice(w_down, (0, here * quarter), (units, quarter))
    parts = [
        lax.dynamic_slice(w_down, (0, (here + k) % quarters * quarter + block * piece), (units, piece))
        for k in range(1, quarters)
    ]
    fetched = jnp.concatenate([shift(part, "etp", k) for k, part in enumerate(parts, 1)], axis=0)
    spread = (
        shift(fetched, "dp", DP_STEP),
        shift(fetched, "dp", -DP_STEP),
        shift(fetched[:, : piece // 2], "dp", 2 * DP_STEP),
        shift(fetched[:, piece // 2 :], "dp", -2 * DP_STEP),
    )
    return own, fetched, *spread


def per_device(tokens, expert_ids, route_weights, w_gate, w_up, w_down):
    tok_rows, width = tokens.shape
    route_count = expert_ids.shape[1]
    sources = lax.axis_size("expert")
    quarters = lax.axis_size("etp")
    experts = sources
    capacity = 2 * tok_rows * route_count // experts
    quarter = width // quarters

    outgoing, combine = dispatch_rows(expert_ids, route_weights, tokens, experts, capacity)
    arrived = lax.all_to_all(
        outgoing.reshape(experts, capacity, width), "expert", split_axis=0, concat_axis=0, tiled=True
    )
    blocks = down_weights(w_down[0], quarter, quarters)
    mine = hidden_units(arrived.reshape(sources * capacity, width), w_gate[0], w_up[0])
    others = [shift(mine, "etp", k) for k in range(1, quarters)]
    expert_out = project_down((mine, *others, *blocks))
    returned = lax.all_to_all(
        expert_out.reshape(sources, capacity, quarter), "expert", split_axis=0, concat_axis=0, tiled=True
    )
    return lax.dot_general(
        combine.reshape(experts * capacity, tok_rows),
        returned.reshape(experts * capacity, quarter),
        (((0,), (0,)), ((), ())),
        preferred_element_type=F32,
    ).astype(BF16)


def solution(mesh):
    return jax.shard_map(
        per_device,
        mesh=mesh,
        in_specs=(
            P(("dp", "expert"), None),
            P(("dp", "expert"), None),
            P(("dp", "expert"), None),
            P("expert", None, "etp"),
            P("expert", None, "etp"),
            P("expert", "etp", None),
        ),
        out_specs=P(("dp", "expert"), "etp"),
        check_vma=False,
    )
```

time: 138 us -> 130 us (0.942)
  waiting for transfers between devices: 70.1 us -> 37 us
  blocking collectives: 0 us -> 22 us
  starting transfers between devices: 47.9 us -> 57.8 us
  other arithmetic: 4.4 us -> 0 us
  Pallas kernels: 12.9 us -> 8.94 us
    all_to_all x1, waiting for transfers between devices: 37.9 us -> 2.61 us  [per_device(): lax.all_to_all(outgoing.reshape(experts, capacity, width), 'expert', spli...]
    ppermute x4 -> x10, waiting for transfers between devices: 4.98 us -> 34.4 us  [shift(): return lax.ppermute(x, axis, [(i, (i + by) % count) for i in range(count)])]
    all_to_all x1 -> x0, waiting for transfers between devices: 27.2 us -> none  [per_device(): lax.all_to_all(expert_out.reshape(sources * quarters, capacity, half), ('...]
    ppermute x4 -> x10, starting transfers between devices: 16 us -> 39.5 us  [shift(): return lax.ppermute(x, axis, [(i, (i + by) % count) for i in range(count)])]
    all_to_all x0 -> x1, blocking collectives: none -> 22 us  [per_device(): lax.all_to_all(expert_out.reshape(sources, capacity, quarter), 'expert',...]
    all_to_all x1 -> x0, starting transfers between devices: 13.4 us -> none  [per_device(): lax.all_to_all(expert_out.reshape(sources * quarters, capacity, half), ('...]
    pallas_call x3 -> x2, Pallas kernels: 8.65 us -> 5.99 us  [the longest x1 4.68 us: hidden_units(): pl.pallas_call(hidden_kernel, out_shape=pltpu.VMEM((rows, units), BF16),...]
    concatenate x3 -> x0, other arithmetic: 2.22 us -> none  [weight_columns(): jnp.concatenate([lax.dynamic_slice(w_down, (0, start + k * 2 * half), (un...]
  transfers between devices with their start and end apart: 6 -> 11, of which waited for: 4 -> 7; matrix products, arithmetic and copies ran while one was open for 4% -> 2% of each run, Pallas kernels for 4% -> 4%
where the time goes in v4:
time: 130 us; the launch traced here: 129 us
  starting transfers between devices  57.8 us (44%)
  waiting for transfers between devices  37 us (28%)
  blocking collectives  22 us (17%)
  Pallas kernels  8.94 us (7%)
  local copies, waits for them, and re-layouts  2.44 us (2%)
    ppermute x10, starting transfers between devices, shift(): return lax.ppermute(x, axis, [(i, (i + by) % count) for i in range(count)])  39.5 us
    ppermute x10, waiting for transfers between devices, shift(): return lax.ppermute(x, axis, [(i, (i + by) % count) for i in range(count)])  34.4 us
    all_to_all x1, blocking collectives, per_device(): lax.all_to_all(expert_out.reshape(sources, capacity, quarter), 'expert',...  22 us
    all_to_all x1, starting transfers between devices, per_device(): lax.all_to_all(outgoing.reshape(experts, capacity, width), 'expert', spli...  18.3 us
    pallas_call x1, Pallas kernels, hidden_units(): pl.pallas_call(hidden_kernel, out_shape=pltpu.VMEM((rows, units), BF16),...  4.68 us
    pallas_call x1, Pallas kernels, dispatch_rows(): pl.pallas_call(dispatch_kernel, grid=(STEPS,), out_shape=(jax.ShapeDtypeS...  2.96 us
    all_to_all x1, waiting for transfers between devices, per_device(): lax.all_to_all(outgoing.reshape(experts, capacity, width), 'expert', spli...  2.61 us
  transfers between devices with their start and end apart: 11, of which 7 were waited for; matrix products, arithmetic and copies ran while one was open for 2% of the time, Pallas kernels for 4%

profile of v4, /device:TPU:1, one launch (start us, length us, event | category | flops | bytes accessed | tf_op | source)
XLA Modules:
  0.0 129.3 jit_solution(7308955427955665019)
XLA Ops:
  0.0 3.0 %shard_map.64 = (bf16[256,4096]{1,0:T(8,128)(2,1)}, bf16[16,16,64]{2,1,0:T(8,128)(2,1)}) custom-call(s32[2,64]{1,0:T(2,128)} %bitcast.25, bf16[2,64]{1,0:T(2,128)(2,1)} %bitcast.26, bf16[64,4096]{1,0:T(8,128)(2,1)} %tokens_ref.1), custom_call_target="tpu_custom_call" | custom-call | flops 134217728 | bytes 2621440 | tf_op jit(solution)/shard_map/pallas_call | solution.py:55
  3.0 18.3 %all-to-all-start = ((bf16[16,16,4096]{2,1,0:T(8,128)(2,1)}), bf16[16,16,4096]{2,1,0:T(8,128)(2,1)}, u32[]{:S(2)}, u32[]{:S(2)}) async-start(bf16[16,16,4096]{2,1,0:T(8,128)(2,1)} %bitcast.24), calls=%async_computation | async-start | bytes 4194304 | tf_op jit(solution)/shard_map/all_to_all | solution.py:196
  21.2 1.2 dynamic-slice_bitcast_fusion.1
  22.4 1.9 %collective-permute-start.3 = (bf16[384,256]{1,0:T(8,128)(2,1)S(1)}, bf16[384,256]{1,0:T(8,128)(2,1)S(1)}, u32[]{:S(2)}, u32[]{:S(2)}) collective-permute-start(bf16[384,256]{1,0:T(8,128)(2,1)S(1)} %get-tuple-element.10), channel_id=1, source_target_pairs={{0,1},{1,2},{2,3},{3,0},{4,5},{5,6},{6,7},{7,4},{8,9},{9,10},{10,1... | collective-permute-start | bytes 589832 | tf_op jit(solution)/shard_map/ppermute | solution.py:20
  24.3 8.2 %collective-permute-start.4 = (bf16[384,256]{1,0:T(8,128)(2,1)S(1)}, bf16[384,256]{1,0:T(8,128)(2,1)S(1)}, u32[]{:S(2)}, u32[]{:S(2)}) collective-permute-start(bf16[384,256]{1,0:T(8,128)(2,1)S(1)} %get-tuple-element.11), channel_id=1, source_target_pairs={{0,2},{1,3},{2,0},{3,1},{4,6},{5,7},{6,4},{7,5},{8,10},{9,11},{10,... | collective-permute-start | bytes 589832 | tf_op jit(solution)/shard_map/ppermute | solution.py:20
  32.5 1.9 %collective-permute-start.5 = (bf16[384,256]{1,0:T(8,128)(2,1)S(1)}, bf16[384,256]{1,0:T(8,128)(2,1)S(1)}, u32[]{:S(2)}, u32[]{:S(2)}) collective-permute-start(bf16[384,256]{1,0:T(8,128)(2,1)S(1)} %get-tuple-element.9), channel_id=1, source_target_pairs={{0,3},{1,0},{2,1},{3,2},{4,7},{5,4},{6,5},{7,6},{8,11},{9,8},{10,9... | collective-permute-start | bytes 589832 | tf_op jit(solution)/shard_map/ppermute | solution.py:20
  34.4 0.0 collective-permute-done.3
  34.5 13.7 %collective-permute-done.4 = bf16[384,256]{1,0:T(8,128)(2,1)S(1)} collective-permute-done((bf16[384,256]{1,0:T(8,128)(2,1)S(1)}, bf16[384,256]{1,0:T(8,128)(2,1)S(1)}, u32[]{:S(2)}, u32[]{:S(2)}) %collective-permute-start.4) | collective-permute-done | bytes 196640 | tf_op jit(solution)/shard_map/ppermute | solution.py:20
  48.2 4.3 %collective-permute-done.5 = bf16[384,256]{1,0:T(8,128)(2,1)S(1)} collective-permute-done((bf16[384,256]{1,0:T(8,128)(2,1)S(1)}, bf16[384,256]{1,0:T(8,128)(2,1)S(1)}, u32[]{:S(2)}, u32[]{:S(2)}) %collective-permute-start.5) | collective-permute-done | bytes 196640 | tf_op jit(solution)/shard_map/ppermute | solution.py:20
  52.4 3.4 %collective-permute-start.6 = (bf16[1152,256]{1,0:T(8,128)(2,1)S(1)}, bf16[1152,256]{1,0:T(8,128)(2,1)S(1)}, u32[]{:S(2)}, u32[]{:S(2)}) collective-permute-start(bf16[1152,256]{1,0:T(8,128)(2,1)S(1)} %constant_dynamic-update-slice_fusion.fetched), channel_id=1, source_target_pairs={{0,128},{64,192},{128,256},{192,320},{256,384},{320,448},{384,512}... | collective-permute-start | bytes 1769480 | tf_op jit(solution)/shard_map/ppermute | solution.py:20
  55.9 4.5 %collective-permute-start.7 = (bf16[1152,256]{1,0:T(8,128)(2,1)S(1)}, bf16[1152,256]{1,0:T(8,128)(2,1)S(1)}, u32[]{:S(2)}, u32[]{:S(2)}) collective-permute-start(bf16[1152,256]{1,0:T(8,128)(2,1)S(1)} %constant_dynamic-update-slice_fusion.fetched), channel_id=1, source_target_pairs={{0,896},{64,960},{128,0},{192,64},{256,128},{320,192},{384,256},{4... | collective-permute-start | bytes 1769480 | tf_op jit(solution)/shard_map/ppermute | solution.py:20
  60.4 1.9 %collective-permute-start.8 = (bf16[1152,128]{1,0:T(8,128)(2,1)S(1)}, bf16[1152,128]{1,0:T(8,128)(2,1)S(1)}, u32[]{:S(2)}, u32[]{:S(2)}) collective-permute-start(bf16[1152,128]{1,0:T(8,128)(2,1)S(1)} %get-tuple-element.13), channel_id=1, source_target_pairs={{0,256},{64,320},{128,384},{192,448},{256,512},{320,576},{384,640}... | collective-permute-start | bytes 884744 | tf_op jit(solution)/shard_map/ppermute | solution.py:20
  62.4 5.5 %collective-permute-start.9 = (bf16[1152,128]{1,0:T(8,128)(2,1)S(1)}, bf16[1152,128]{1,0:T(8,128)(2,1)S(1)}, u32[]{:S(2)}, u32[]{:S(2)}) collective-permute-start(bf16[1152,128]{1,0:T(8,128)(2,1)S(1)} %get-tuple-element.12), channel_id=1, source_target_pairs={{0,768},{64,832},{128,896},{192,960},{256,0},{320,64},{384,128},{4... | collective-permute-start | bytes 884744 | tf_op jit(solution)/shard_map/ppermute | solution.py:20
  67.8 2.6 %all-to-all-done = bf16[16,16,4096]{2,1,0:T(8,128)(2,1)} async-done(((bf16[16,16,4096]{2,1,0:T(8,128)(2,1)}), bf16[16,16,4096]{2,1,0:T(8,128)(2,1)}, u32[]{:S(2)}, u32[]{:S(2)}) %all-to-all-start) | async-done | bytes 2097184 | tf_op jit(solution)/shard_map/all_to_all | solution.py:196
  70.5 4.7 %shard_map.65.mine = bf16[256,384]{1,0:T(8,128)(2,1)S(1)} custom-call(bf16[256,4096]{1,0:T(8,128)(2,1)} %bitcast.3.x_ref, bf16[4096,384]{1,0:T(8,128)(2,1)} %bitcast.22, bf16[4096,384]{1,0:T(8,128)(2,1)} %bitcast.23), custom_call_target="tpu_custom_call" | custom-call | flops 1610612736 | bytes 8585216 | tf_op jit(solution)/shard_map/pallas_call | solution.py:111
  75.1 1.9 %collective-permute-start = (bf16[256,384]{1,0:T(8,128)(2,1)S(1)}, bf16[256,384]{1,0:T(8,128)(2,1)S(1)}, u32[]{:S(2)}, u32[]{:S(2)}) collective-permute-start(bf16[256,384]{1,0:T(8,128)(2,1)S(1)} %shard_map.65.mine), channel_id=1, source_target_pairs={{0,1},{1,2},{2,3},{3,0},{4,5},{5,6},{6,7},{7,4},{8,9},{9,10},{10,1... | collective-permute-start | bytes 589832 | tf_op jit(solution)/shard_map/ppermute | solution.py:20
  77.1 3.1 %collective-permute-done.8.low = bf16[1152,128]{1,0:T(8,128)(2,1)S(1)} collective-permute-done((bf16[1152,128]{1,0:T(8,128)(2,1)S(1)}, bf16[1152,128]{1,0:T(8,128)(2,1)S(1)}, u32[]{:S(2)}, u32[]{:S(2)}) %collective-permute-start.8) | collective-permute-done | bytes 294944 | tf_op jit(solution)/shard_map/ppermute | solution.py:20
  80.2 5.0 %collective-permute-start.1 = (bf16[256,384]{1,0:T(8,128)(2,1)S(1)}, bf16[256,384]{1,0:T(8,128)(2,1)S(1)}, u32[]{:S(2)}, u32[]{:S(2)}) collective-permute-start(bf16[256,384]{1,0:T(8,128)(2,1)S(1)} %shard_map.65.mine), channel_id=1, source_target_pairs={{0,2},{1,3},{2,0},{3,1},{4,6},{5,7},{6,4},{7,5},{8,10},{9,11},{10,... | collective-permute-start | bytes 589832 | tf_op jit(solution)/shard_map/ppermute | solution.py:20
  85.2 0.5 collective-permute-done.9.high
  85.7 5.3 %collective-permute-start.2 = (bf16[256,384]{1,0:T(8,128)(2,1)S(1)}, bf16[256,384]{1,0:T(8,128)(2,1)S(1)}, u32[]{:S(2)}, u32[]{:S(2)}) collective-permute-start(bf16[256,384]{1,0:T(8,128)(2,1)S(1)} %shard_map.65.mine), channel_id=1, source_target_pairs={{0,3},{1,0},{2,1},{3,2},{4,7},{5,4},{6,5},{7,6},{8,11},{9,8},{10,9... | collective-permute-start | bytes 589832 | tf_op jit(solution)/shard_map/ppermute | solution.py:20
  91.0 1.2 dynamic-slice_bitcast_fusion.own
  92.2 0.0 copy-start
  92.2 0.0 collective-permute-done.6.left
  92.2 0.0 collective-permute-done.7.right
  92.2 0.0 collective-permute-done.other1
  92.2 8.5 %collective-permute-done.1.other2 = bf16[256,384]{1,0:T(8,128)(2,1)S(1)} collective-permute-done((bf16[256,384]{1,0:T(8,128)(2,1)S(1)}, bf16[256,384]{1,0:T(8,128)(2,1)S(1)}, u32[]{:S(2)}, u32[]{:S(2)}) %collective-permute-start.1) | collective-permute-done | bytes 196640 | tf_op jit(solution)/shard_map/ppermute | solution.py:20
  100.7 4.4 %collective-permute-done.2.other3 = bf16[256,384]{1,0:T(8,128)(2,1)S(1)} collective-permute-done((bf16[256,384]{1,0:T(8,128)(2,1)S(1)}, bf16[256,384]{1,0:T(8,128)(2,1)S(1)}, u32[]{:S(2)}, u32[]{:S(2)}) %collective-permute-start.2) | collective-permute-done | bytes 196640 | tf_op jit(solution)/shard_map/ppermute | solution.py:20
  105.0 1.3 %shard_map.66 = bf16[256,1024]{1,0:T(8,128)(2,1)S(1)} custom-call(bf16[256,384]{1,0:T(8,128)(2,1)S(1)} %shard_map.65.mine, bf16[256,384]{1,0:T(8,128)(2,1)S(1)} %collective-permute-done.other1, bf16[256,384]{1,0:T(8,128)(2,1)S(1)} %collective-permute-done.1.other2, bf16[256,384]{1,0:T(8,128)(2,1)S(1)} %collective-permute-done.2.other3, ...), custom_call_target="tpu_custom_call" | custom-call | flops 805306368 | bytes 4456448 | tf_op jit(solution)/shard_map/pallas_call | solution.py:153
  106.3 22.0 %all_to_all.10 = bf16[16,16,1024]{2,1,0:T(8,128)(2,1)S(1)} all-to-all(bf16[16,16,1024]{2,1,0:T(8,128)(2,1)S(1)} %bitcast.21), channel_id=1, replica_groups=mesh['dp'=16,'expert'=16,'etp'=4] {'expert'}, dimensions={0} | all-to-all | bytes 1048576 | tf_op jit(solution)/shard_map/all_to_all | solution.py:203
  128.4 0.0 copy-done
  128.4 0.9 fusion
  (4 shorter events, 0.1 us)
Async XLA Ops:
  3.0 67.5 %all-to-all-start = ((bf16[16,16,4096]{2,1,0:T(8,128)(2,1)}), bf16[16,16,4096]{2,1,0:T(8,128)(2,1)}, u32[]{:S(2)}, u32[]{:S(2)}) async-start(bf16[16,16,4096]{2,1,0:T(8,128)(2,1)} %bitcast.24), calls=%async_computation | async-start | bytes 4194304 | tf_op jit(solution)/shard_map/all_to_all | solution.py:196
  22.4 12.0 %collective-permute-start.3 = (bf16[384,256]{1,0:T(8,128)(2,1)S(1)}, bf16[384,256]{1,0:T(8,128)(2,1)S(1)}, u32[]{:S(2)}, u32[]{:S(2)}) collective-permute-start(bf16[384,256]{1,0:T(8,128)(2,1)S(1)} %get-tuple-element.10), channel_id=1, source_target_pairs={{0,1},{1,2},{2,3},{3,0},{4,5},{5,6},{6,7},{7,4},{8,9},{9,10},{10,1... | collective-permute-start | bytes 589832 | tf_op jit(solution)/shard_map/ppermute | solution.py:20
  24.3 23.8 %collective-permute-start.4 = (bf16[384,256]{1,0:T(8,128)(2,1)S(1)}, bf16[384,256]{1,0:T(8,128)(2,1)S(1)}, u32[]{:S(2)}, u32[]{:S(2)}) collective-permute-start(bf16[384,256]{1,0:T(8,128)(2,1)S(1)} %get-tuple-element.11), channel_id=1, source_target_pairs={{0,2},{1,3},{2,0},{3,1},{4,6},{5,7},{6,4},{7,5},{8,10},{9,11},{10,... | collective-permute-start | bytes 589832 | tf_op jit(solution)/shard_map/ppermute | solution.py:20
  32.5 19.9 %collective-permute-start.5 = (bf16[384,256]{1,0:T(8,128)(2,1)S(1)}, bf16[384,256]{1,0:T(8,128)(2,1)S(1)}, u32[]{:S(2)}, u32[]{:S(2)}) collective-permute-start(bf16[384,256]{1,0:T(8,128)(2,1)S(1)} %get-tuple-element.9), channel_id=1, source_target_pairs={{0,3},{1,0},{2,1},{3,2},{4,7},{5,4},{6,5},{7,6},{8,11},{9,8},{10,9... | collective-permute-start | bytes 589832 | tf_op jit(solution)/shard_map/ppermute | solution.py:20
  52.4 39.8 %collective-permute-start.6 = (bf16[1152,256]{1,0:T(8,128)(2,1)S(1)}, bf16[1152,256]{1,0:T(8,128)(2,1)S(1)}, u32[]{:S(2)}, u32[]{:S(2)}) collective-permute-start(bf16[1152,256]{1,0:T(8,128)(2,1)S(1)} %constant_dynamic-update-slice_fusion.fetched), channel_id=1, source_target_pairs={{0,128},{64,192},{128,256},{192,320},{256,384},{320,448},{384,512}... | collective-permute-start | bytes 1769480 | tf_op jit(solution)/shard_map/ppermute | solution.py:20
  55.9 36.3 %collective-permute-start.7 = (bf16[1152,256]{1,0:T(8,128)(2,1)S(1)}, bf16[1152,256]{1,0:T(8,128)(2,1)S(1)}, u32[]{:S(2)}, u32[]{:S(2)}) collective-permute-start(bf16[1152,256]{1,0:T(8,128)(2,1)S(1)} %constant_dynamic-update-slice_fusion.fetched), channel_id=1, source_target_pairs={{0,896},{64,960},{128,0},{192,64},{256,128},{320,192},{384,256},{4... | collective-permute-start | bytes 1769480 | tf_op jit(solution)/shard_map/ppermute | solution.py:20
  60.4 19.7 %collective-permute-start.8 = (bf16[1152,128]{1,0:T(8,128)(2,1)S(1)}, bf16[1152,128]{1,0:T(8,128)(2,1)S(1)}, u32[]{:S(2)}, u32[]{:S(2)}) collective-permute-start(bf16[1152,128]{1,0:T(8,128)(2,1)S(1)} %get-tuple-element.13), channel_id=1, source_target_pairs={{0,256},{64,320},{128,384},{192,448},{256,512},{320,576},{384,640}... | collective-permute-start | bytes 884744 | tf_op jit(solution)/shard_map/ppermute | solution.py:20
  62.4 23.3 %collective-permute-start.9 = (bf16[1152,128]{1,0:T(8,128)(2,1)S(1)}, bf16[1152,128]{1,0:T(8,128)(2,1)S(1)}, u32[]{:S(2)}, u32[]{:S(2)}) collective-permute-start(bf16[1152,128]{1,0:T(8,128)(2,1)S(1)} %get-tuple-element.12), channel_id=1, source_target_pairs={{0,768},{64,832},{128,896},{192,960},{256,0},{320,64},{384,128},{4... | collective-permute-start | bytes 884744 | tf_op jit(solution)/shard_map/ppermute | solution.py:20
  75.1 17.1 %collective-permute-start = (bf16[256,384]{1,0:T(8,128)(2,1)S(1)}, bf16[256,384]{1,0:T(8,128)(2,1)S(1)}, u32[]{:S(2)}, u32[]{:S(2)}) collective-permute-start(bf16[256,384]{1,0:T(8,128)(2,1)S(1)} %shard_map.65.mine), channel_id=1, source_target_pairs={{0,1},{1,2},{2,3},{3,0},{4,5},{5,6},{6,7},{7,4},{8,9},{9,10},{10,1... | collective-permute-start | bytes 589832 | tf_op jit(solution)/shard_map/ppermute | solution.py:20
  80.2 20.5 %collective-permute-start.1 = (bf16[256,384]{1,0:T(8,128)(2,1)S(1)}, bf16[256,384]{1,0:T(8,128)(2,1)S(1)}, u32[]{:S(2)}, u32[]{:S(2)}) collective-permute-start(bf16[256,384]{1,0:T(8,128)(2,1)S(1)} %shard_map.65.mine), channel_id=1, source_target_pairs={{0,2},{1,3},{2,0},{3,1},{4,6},{5,7},{6,4},{7,5},{8,10},{9,11},{10,... | collective-permute-start | bytes 589832 | tf_op jit(solution)/shard_map/ppermute | solution.py:20
  85.7 19.3 %collective-permute-start.2 = (bf16[256,384]{1,0:T(8,128)(2,1)S(1)}, bf16[256,384]{1,0:T(8,128)(2,1)S(1)}, u32[]{:S(2)}, u32[]{:S(2)}) collective-permute-start(bf16[256,384]{1,0:T(8,128)(2,1)S(1)} %shard_map.65.mine), channel_id=1, source_target_pairs={{0,3},{1,0},{2,1},{3,2},{4,7},{5,4},{6,5},{7,6},{8,11},{9,8},{10,9... | collective-permute-start | bytes 589832 | tf_op jit(solution)/shard_map/ppermute | solution.py:20
  92.2 36.2 %copy-start = (bf16[16,16,64]{2,1,0:T(8,128)(2,1)S(1)}, bf16[16,16,64]{2,1,0:T(8,128)(2,1)}, u32[]{:S(2)}) copy-start(bf16[16,16,64]{2,1,0:T(8,128)(2,1)} %get-tuple-element.7) | copy-start | bytes 98308

commit v5 on v4

--- a/solution.py
+++ b/solution.py
@@ -127,14 +127,18 @@
     )(arrived, w_gate, w_up)
 
 
-def down_kernel(mine, other1, other2, other3, own, fetched, left, right, low, high, out_ref):
+def down_kernel(hidden, own, fetched, left, right, low, high, out_ref):
     piece, side = fetched.shape[1], low.shape[1]
     here = lax.rem(lax.div(lax.axis_index("dp"), DP_STEP), SHARERS)
-    others = jnp.concatenate([other1[...], other2[...], other3[...]], axis=1)
+    groups, group = hidden.shape[0], lax.axis_index("etp")
+    mine = hidden[group]
+    others = jnp.concatenate(
+        [hidden[lax.rem(group + groups - k, groups)] for k in range(1, groups)], axis=1
+    )
 
     def project(start, block):
         columns = pl.ds(pl.multiple_of(start, side), block.shape[1])
-        total = jnp.dot(mine[...], own[:, columns], preferred_element_type=F32)
+        total = jnp.dot(mine, own[:, columns], preferred_element_type=F32)
         total += jnp.dot(others, block[...], preferred_element_type=F32)
         out_ref[:, columns] = total.astype(out_ref.dtype)
 
@@ -147,9 +151,8 @@
 
 
 def project_down(operands):
-    rows, units = operands[0].shape
-    own = operands[4]
-    quarter = own.shape[1]
+    groups, rows, units = operands[0].shape
+    quarter = operands[1].shape[1]
     return pl.pallas_call(
         down_kernel,
         out_shape=jax.ShapeDtypeStruct((rows, quarter), BF16),
@@ -157,8 +160,8 @@
         out_specs=IN_VMEM,
         compiler_params=pltpu.CompilerParams(vmem_limit_bytes=16 * 2**20),
         cost_estimate=pl.CostEstimate(
-            flops=8 * rows * units * quarter,
-            bytes_accessed=8 * (rows * units + units * quarter) + 2 * rows * quarter,
+            flops=2 * groups * rows * units * quarter,
+            bytes_accessed=2 * groups * (rows * units + units * quarter) + 2 * rows * quarter,
             transcendentals=0,
         ),
     )(*operands)
@@ -198,8 +201,8 @@
     )
     blocks = down_weights(w_down[0], quarter, quarters)
     mine = hidden_units(arrived.reshape(sources * capacity, width), w_gate[0], w_up[0])
-    others = [shift(mine, "etp", k) for k in range(1, quarters)]
-    expert_out = project_down((mine, *others, *blocks))
+    gathered = lax.all_gather(mine, "etp")
+    expert_out = project_down((gathered, *blocks))
     returned = lax.all_to_all(
         expert_out.reshape(sources, capacity, quarter), "expert", split_axis=0, concat_axis=0, tiled=True
     )

time: 130 us -> 121 us (0.931)
  blocking collectives: 22 us -> 43.3 us
  waiting for transfers between devices: 37 us -> 18.7 us
  starting transfers between devices: 57.8 us -> 45.6 us
    all_gather x0 -> x1, blocking collectives: none -> 18.8 us  [per_device(): gathered = lax.all_gather(mine, 'etp')]
    ppermute x10 -> x7, waiting for transfers between devices: 34.4 us -> 16.8 us  [shift(): return lax.ppermute(x, axis, [(i, (i + by) % count) for i in range(count)])]
    ppermute x10 -> x7, starting transfers between devices: 39.5 us -> 27.3 us  [shift(): return lax.ppermute(x, axis, [(i, (i + by) % count) for i in range(count)])]
    all_to_all x1, blocking collectives: 22 us -> 24.5 us  [per_device(): lax.all_to_all(expert_out.reshape(sources, capacity, quarter), 'expert',...]
  transfers between devices with their start and end apart: 11 -> 8, of which waited for: 7 -> 3; matrix products, arithmetic and copies ran while one was open for 2% -> 3% of each run, Pallas kernels for 4% -> 4%
where the time goes in v5:
time: 121 us
  starting transfers between devices  45.6 us (38%)
  blocking collectives  43.3 us (36%)
  waiting for transfers between devices  18.7 us (15%)
  Pallas kernels  9.03 us (7%)
  local copies, waits for them, and re-layouts  3.16 us (3%)
    ppermute x7, starting transfers between devices, shift(): return lax.ppermute(x, axis, [(i, (i + by) % count) for i in range(count)])  27.3 us
    all_to_all x1, blocking collectives, per_device(): lax.all_to_all(expert_out.reshape(sources, capacity, quarter), 'expert',...  24.5 us
    all_gather x1, blocking collectives, per_device(): gathered = lax.all_gather(mine, 'etp')  18.8 us
    all_to_all x1, starting transfers between devices, per_device(): lax.all_to_all(outgoing.reshape(experts, capacity, width), 'expert', spli...  18.3 us
    ppermute x7, waiting for transfers between devices, shift(): return lax.ppermute(x, axis, [(i, (i + by) % count) for i in range(count)])  16.8 us
    pallas_call x1, Pallas kernels, hidden_units(): pl.pallas_call(hidden_kernel, out_shape=pltpu.VMEM((rows, units), BF16),...  4.68 us
    pallas_call x1, Pallas kernels, dispatch_rows(): pl.pallas_call(dispatch_kernel, grid=(STEPS,), out_shape=(jax.ShapeDtypeS...  3.03 us
  transfers between devices with their start and end apart: 8, of which 3 were waited for; matrix products, arithmetic and copies ran while one was open for 3% of the time, Pallas kernels for 4%

profile of v5, /device:TPU:1, one launch (start us, length us, event | category | flops | bytes accessed | tf_op | source)
XLA Modules:
  0.0 120.7 jit_solution(12214615297429925879)
XLA Ops:
  0.0 3.0 %shard_map.64 = (bf16[256,4096]{1,0:T(8,128)(2,1)}, bf16[16,16,64]{2,1,0:T(8,128)(2,1)}) custom-call(s32[2,64]{1,0:T(2,128)} %bitcast.27, bf16[2,64]{1,0:T(2,128)(2,1)} %bitcast.28, bf16[64,4096]{1,0:T(8,128)(2,1)} %tokens_ref.1), custom_call_target="tpu_custom_call" | custom-call | flops 134217728 | bytes 2621440 | tf_op jit(solution)/shard_map/pallas_call | solution.py:55
  3.0 18.3 %all-to-all-start = ((bf16[16,16,4096]{2,1,0:T(8,128)(2,1)}), bf16[16,16,4096]{2,1,0:T(8,128)(2,1)}, u32[]{:S(2)}, u32[]{:S(2)}) async-start(bf16[16,16,4096]{2,1,0:T(8,128)(2,1)} %bitcast.26), calls=%async_computation | async-start | bytes 4194304 | tf_op jit(solution)/shard_map/all_to_all | solution.py:199
  21.3 1.2 dynamic-slice_bitcast_fusion.1
  22.5 1.9 %collective-permute-start = (bf16[384,256]{1,0:T(8,128)(2,1)S(1)}, bf16[384,256]{1,0:T(8,128)(2,1)S(1)}, u32[]{:S(2)}, u32[]{:S(2)}) collective-permute-start(bf16[384,256]{1,0:T(8,128)(2,1)S(1)} %get-tuple-element.10), channel_id=1, source_target_pairs={{0,1},{1,2},{2,3},{3,0},{4,5},{5,6},{6,7},{7,4},{8,9},{9,10},{10,1... | collective-permute-start | bytes 589832 | tf_op jit(solution)/shard_map/ppermute | solution.py:20
  24.4 8.2 %collective-permute-start.1 = (bf16[384,256]{1,0:T(8,128)(2,1)S(1)}, bf16[384,256]{1,0:T(8,128)(2,1)S(1)}, u32[]{:S(2)}, u32[]{:S(2)}) collective-permute-start(bf16[384,256]{1,0:T(8,128)(2,1)S(1)} %get-tuple-element.11), channel_id=1, source_target_pairs={{0,2},{1,3},{2,0},{3,1},{4,6},{5,7},{6,4},{7,5},{8,10},{9,11},{10,... | collective-permute-start | bytes 589832 | tf_op jit(solution)/shard_map/ppermute | solution.py:20
  32.6 1.9 %collective-permute-start.2 = (bf16[384,256]{1,0:T(8,128)(2,1)S(1)}, bf16[384,256]{1,0:T(8,128)(2,1)S(1)}, u32[]{:S(2)}, u32[]{:S(2)}) collective-permute-start(bf16[384,256]{1,0:T(8,128)(2,1)S(1)} %get-tuple-element.9), channel_id=1, source_target_pairs={{0,3},{1,0},{2,1},{3,2},{4,7},{5,4},{6,5},{7,6},{8,11},{9,8},{10,9... | collective-permute-start | bytes 589832 | tf_op jit(solution)/shard_map/ppermute | solution.py:20
  34.5 1.2 dynamic-slice_bitcast_fusion.own
  35.7 0.0 collective-permute-done
  35.7 12.5 %collective-permute-done.1 = bf16[384,256]{1,0:T(8,128)(2,1)S(1)} collective-permute-done((bf16[384,256]{1,0:T(8,128)(2,1)S(1)}, bf16[384,256]{1,0:T(8,128)(2,1)S(1)}, u32[]{:S(2)}, u32[]{:S(2)}) %collective-permute-start.1) | collective-permute-done | bytes 196640 | tf_op jit(solution)/shard_map/ppermute | solution.py:20
  48.2 4.3 %collective-permute-done.2 = bf16[384,256]{1,0:T(8,128)(2,1)S(1)} collective-permute-done((bf16[384,256]{1,0:T(8,128)(2,1)S(1)}, bf16[384,256]{1,0:T(8,128)(2,1)S(1)}, u32[]{:S(2)}, u32[]{:S(2)}) %collective-permute-start.2) | collective-permute-done | bytes 196640 | tf_op jit(solution)/shard_map/ppermute | solution.py:20
  52.5 3.4 %collective-permute-start.3 = (bf16[1152,256]{1,0:T(8,128)(2,1)S(1)}, bf16[1152,256]{1,0:T(8,128)(2,1)S(1)}, u32[]{:S(2)}, u32[]{:S(2)}) collective-permute-start(bf16[1152,256]{1,0:T(8,128)(2,1)S(1)} %constant_dynamic-update-slice_fusion.fetched), channel_id=1, source_target_pairs={{0,128},{64,192},{128,256},{192,320},{256,384},{320,448},{384,512}... | collective-permute-start | bytes 1769480 | tf_op jit(solution)/shard_map/ppermute | solution.py:20
  56.0 4.5 %collective-permute-start.4 = (bf16[1152,256]{1,0:T(8,128)(2,1)S(1)}, bf16[1152,256]{1,0:T(8,128)(2,1)S(1)}, u32[]{:S(2)}, u32[]{:S(2)}) collective-permute-start(bf16[1152,256]{1,0:T(8,128)(2,1)S(1)} %constant_dynamic-update-slice_fusion.fetched), channel_id=1, source_target_pairs={{0,896},{64,960},{128,0},{192,64},{256,128},{320,192},{384,256},{4... | collective-permute-start | bytes 1769480 | tf_op jit(solution)/shard_map/ppermute | solution.py:20
  60.5 0.8 fusion.1
  61.2 1.9 %collective-permute-start.5 = (bf16[1152,128]{1,0:T(8,128)(2,1)}, bf16[1152,128]{1,0:T(8,128)(2,1)S(1)}, u32[]{:S(2)}, u32[]{:S(2)}) collective-permute-start(bf16[1152,128]{1,0:T(8,128)(2,1)} %get-tuple-element.13), channel_id=1, source_target_pairs={{0,256},{64,320},{128,384},{192,448},{256,512},{320,576},{384,640}... | collective-permute-start | bytes 884744 | tf_op jit(solution)/shard_map/ppermute | solution.py:20
  63.1 5.5 %collective-permute-start.6 = (bf16[1152,128]{1,0:T(8,128)(2,1)S(1)}, bf16[1152,128]{1,0:T(8,128)(2,1)S(1)}, u32[]{:S(2)}, u32[]{:S(2)}) collective-permute-start(bf16[1152,128]{1,0:T(8,128)(2,1)S(1)} %get-tuple-element.12), channel_id=1, source_target_pairs={{0,768},{64,832},{128,896},{192,960},{256,0},{320,64},{384,128},{4... | collective-permute-start | bytes 884744 | tf_op jit(solution)/shard_map/ppermute | solution.py:20
  68.6 1.9 %all-to-all-done = bf16[16,16,4096]{2,1,0:T(8,128)(2,1)} async-done(((bf16[16,16,4096]{2,1,0:T(8,128)(2,1)}), bf16[16,16,4096]{2,1,0:T(8,128)(2,1)}, u32[]{:S(2)}, u32[]{:S(2)}) %all-to-all-start) | async-done | bytes 2097184 | tf_op jit(solution)/shard_map/all_to_all | solution.py:199
  70.5 4.7 %shard_map.65 = bf16[256,384]{1,0:T(8,128)(2,1)S(1)} custom-call(bf16[256,4096]{1,0:T(8,128)(2,1)} %bitcast.3.x_ref, bf16[4096,384]{1,0:T(8,128)(2,1)} %bitcast.24, bf16[4096,384]{1,0:T(8,128)(2,1)} %bitcast.25), custom_call_target="tpu_custom_call" | custom-call | flops 1610612736 | bytes 8585216 | tf_op jit(solution)/shard_map/pallas_call | solution.py:111
  75.2 0.0 copy-start
  75.2 18.8 %all-gather = bf16[1024,384]{1,0:T(8,128)(2,1)S(1)} all-gather(bf16[256,384]{1,0:T(8,128)(2,1)S(1)} %shard_map.65), channel_id=2, replica_groups=mesh['dp'=16,'expert'=16,'etp'=4] {'etp'}, dimensions={0}, use_global_device_ids=true | all-gather | bytes 983040 | tf_op jit(solution)/shard_map/all_gather | solution.py:204
  94.1 0.0 collective-permute-done.5.low
  94.1 0.0 collective-permute-done.6.high
  94.1 0.0 collective-permute-done.3.left
  94.1 0.0 collective-permute-done.4.right
  94.1 1.3 %shard_map.66 = bf16[256,1024]{1,0:T(8,128)(2,1)S(1)} custom-call(bf16[4,256,384]{2,1,0:T(8,128)(2,1)S(1)} %bitcast.22, bf16[384,1024]{1,0:T(8,128)(2,1)S(1)} %dynamic-slice_bitcast_fusion.own, bf16[1152,256]{1,0:T(8,128)(2,1)S(1)} %constant_dynamic-update-slice_fusion.fetched, bf16[1152,256]{1,0:T(8,128)(2,1)S(1)} %collective-permute-done.3.left, ...), custom_call_target="tpu_custom_call" | custom-call | flops 805306368 | bytes 4456448 | tf_op jit(solution)/shard_map/pallas_call | solution.py:156
  95.4 24.5 %all_to_all.10 = bf16[16,16,1024]{2,1,0:T(8,128)(2,1)S(1)} all-to-all(bf16[16,16,1024]{2,1,0:T(8,128)(2,1)S(1)} %bitcast.23), channel_id=1, replica_groups=mesh['dp'=16,'expert'=16,'etp'=4] {'expert'}, dimensions={0} | all-to-all | bytes 1048576 | tf_op jit(solution)/shard_map/all_to_all | solution.py:206
  119.9 0.0 copy-done
  119.9 0.9 fusion
  (3 shorter events, 0.0 us)
Async XLA Ops:
  3.0 67.5 %all-to-all-start = ((bf16[16,16,4096]{2,1,0:T(8,128)(2,1)}), bf16[16,16,4096]{2,1,0:T(8,128)(2,1)}, u32[]{:S(2)}, u32[]{:S(2)}) async-start(bf16[16,16,4096]{2,1,0:T(8,128)(2,1)} %bitcast.26), calls=%async_computation | async-start | bytes 4194304 | tf_op jit(solution)/shard_map/all_to_all | solution.py:199
  22.5 13.2 %collective-permute-start = (bf16[384,256]{1,0:T(8,128)(2,1)S(1)}, bf16[384,256]{1,0:T(8,128)(2,1)S(1)}, u32[]{:S(2)}, u32[]{:S(2)}) collective-permute-start(bf16[384,256]{1,0:T(8,128)(2,1)S(1)} %get-tuple-element.10), channel_id=1, source_target_pairs={{0,1},{1,2},{2,3},{3,0},{4,5},{5,6},{6,7},{7,4},{8,9},{9,10},{10,1... | collective-permute-start | bytes 589832 | tf_op jit(solution)/shard_map/ppermute | solution.py:20
  24.4 23.8 %collective-permute-start.1 = (bf16[384,256]{1,0:T(8,128)(2,1)S(1)}, bf16[384,256]{1,0:T(8,128)(2,1)S(1)}, u32[]{:S(2)}, u32[]{:S(2)}) collective-permute-start(bf16[384,256]{1,0:T(8,128)(2,1)S(1)} %get-tuple-element.11), channel_id=1, source_target_pairs={{0,2},{1,3},{2,0},{3,1},{4,6},{5,7},{6,4},{7,5},{8,10},{9,11},{10,... | collective-permute-start | bytes 589832 | tf_op jit(solution)/shard_map/ppermute | solution.py:20
  32.6 19.9 %collective-permute-start.2 = (bf16[384,256]{1,0:T(8,128)(2,1)S(1)}, bf16[384,256]{1,0:T(8,128)(2,1)S(1)}, u32[]{:S(2)}, u32[]{:S(2)}) collective-permute-start(bf16[384,256]{1,0:T(8,128)(2,1)S(1)} %get-tuple-element.9), channel_id=1, source_target_pairs={{0,3},{1,0},{2,1},{3,2},{4,7},{5,4},{6,5},{7,6},{8,11},{9,8},{10,9... | collective-permute-start | bytes 589832 | tf_op jit(solution)/shard_map/ppermute | solution.py:20
  52.5 41.5 %collective-permute-start.3 = (bf16[1152,256]{1,0:T(8,128)(2,1)S(1)}, bf16[1152,256]{1,0:T(8,128)(2,1)S(1)}, u32[]{:S(2)}, u32[]{:S(2)}) collective-permute-start(bf16[1152,256]{1,0:T(8,128)(2,1)S(1)} %constant_dynamic-update-slice_fusion.fetched), channel_id=1, source_target_pairs={{0,128},{64,192},{128,256},{192,320},{256,384},{320,448},{384,512}... | collective-permute-start | bytes 1769480 | tf_op jit(solution)/shard_map/ppermute | solution.py:20
  56.0 38.1 %collective-permute-start.4 = (bf16[1152,256]{1,0:T(8,128)(2,1)S(1)}, bf16[1152,256]{1,0:T(8,128)(2,1)S(1)}, u32[]{:S(2)}, u32[]{:S(2)}) collective-permute-start(bf16[1152,256]{1,0:T(8,128)(2,1)S(1)} %constant_dynamic-update-slice_fusion.fetched), channel_id=1, source_target_pairs={{0,896},{64,960},{128,0},{192,64},{256,128},{320,192},{384,256},{4... | collective-permute-start | bytes 1769480 | tf_op jit(solution)/shard_map/ppermute | solution.py:20
  61.2 32.8 %collective-permute-start.5 = (bf16[1152,128]{1,0:T(8,128)(2,1)}, bf16[1152,128]{1,0:T(8,128)(2,1)S(1)}, u32[]{:S(2)}, u32[]{:S(2)}) collective-permute-start(bf16[1152,128]{1,0:T(8,128)(2,1)} %get-tuple-element.13), channel_id=1, source_target_pairs={{0,256},{64,320},{128,384},{192,448},{256,512},{320,576},{384,640}... | collective-permute-start | bytes 884744 | tf_op jit(solution)/shard_map/ppermute | solution.py:20
  63.1 30.9 %collective-permute-start.6 = (bf16[1152,128]{1,0:T(8,128)(2,1)S(1)}, bf16[1152,128]{1,0:T(8,128)(2,1)S(1)}, u32[]{:S(2)}, u32[]{:S(2)}) collective-permute-start(bf16[1152,128]{1,0:T(8,128)(2,1)S(1)} %get-tuple-element.12), channel_id=1, source_target_pairs={{0,768},{64,832},{128,896},{192,960},{256,0},{320,64},{384,128},{4... | collective-permute-start | bytes 884744 | tf_op jit(solution)/shard_map/ppermute | solution.py:20
  75.2 44.6 %copy-start = (bf16[16,16,64]{2,1,0:T(8,128)(2,1)S(1)}, bf16[16,16,64]{2,1,0:T(8,128)(2,1)}, u32[]{:S(2)}) copy-start(bf16[16,16,64]{2,1,0:T(8,128)(2,1)} %get-tuple-element.7) | copy-start | bytes 98308

commit v6 on v5

--- a/solution.py
+++ b/solution.py
@@ -6,8 +6,8 @@
 from jax.sharding import PartitionSpec as P
 
 
-STEPS = 2
-PIECES = 4
+STEPS = 8
+PIECES = (1, 3, 3, 3, 3, 3)
 DP_STEP = 2
 SHARERS = 4
 BF16, F32 = jnp.bfloat16, jnp.float32
@@ -20,51 +20,70 @@
     return lax.ppermute(x, axis, [(i, (i + by) % count) for i in range(count)])
 
 
-def dispatch_kernel(ids_ref, weights_ref, tokens_ref, out_ref, combine_ref, chosen):
-    experts, capacity = combine_ref.shape[0], combine_ref.shape[1]
-    routes, rows = ids_ref.shape
-
-    @pl.when(pl.program_id(0) == 0)
-    def _():
-        expert = lax.broadcasted_iota(jnp.int32, (experts, rows), 0)
-        named = jnp.zeros((experts, rows), F32)
-        weight = jnp.zeros((experts, rows), F32)
-        for k in range(routes):
-            hit = ids_ref[k : k + 1, :] == expert
-            named = jnp.where(hit, 1.0, named)
-            weight = jnp.where(hit, weights_ref[k : k + 1, :].astype(F32), weight)
-        earlier = lax.broadcasted_iota(jnp.int32, (rows, rows), 0) < lax.broadcasted_iota(
-            jnp.int32, (rows, rows), 1
-        )
-        slot = jnp.dot(
-            named.astype(BF16), jnp.where(earlier, 1.0, 0.0).astype(BF16), preferred_element_type=F32
-        ).astype(jnp.int32)
-        slot = jnp.where(named > 0.0, slot, -1)
-        place = lax.broadcasted_iota(jnp.int32, (experts, capacity, rows), 1)
-        taken = slot[:, None, :] == place
-        chosen[...] = jnp.where(taken, 1.0, 0.0).reshape(experts * capacity, rows).astype(BF16)
-        combine_ref[...] = jnp.where(taken, weight[:, None, :], 0.0).astype(BF16)
-
-    out_ref[...] = jnp.dot(chosen[...], tokens_ref[...], preferred_element_type=F32).astype(BF16)
+def dispatch_kernel(
+    ids_ref, weights_ref, tokens_ref, out_ref, combine_ref, ids, weights, tokens, out, combine, sems
+):
+    experts, capacity, rows = combine.shape
+    routes, width = ids.shape[0], tokens.shape[1]
+    reads = (
+        pltpu.make_async_copy(ids_ref, ids, sems.at[0]),
+        pltpu.make_async_copy(weights_ref, weights, sems.at[1]),
+        pltpu.make_async_copy(tokens_ref, tokens, sems.at[2]),
+    )
+    for copy in reads:
+        copy.start()
+    expert = lax.broadcasted_iota(jnp.int32, (experts, rows), 0)
+    place = lax.broadcasted_iota(jnp.int32, (experts, capacity, rows), 1)
+    earlier = lax.broadcasted_iota(jnp.int32, (rows, rows), 0) < lax.broadcasted_iota(
+        jnp.int32, (rows, rows), 1
+    )
+    reads[0].wait()
+    named = jnp.zeros((experts, rows), F32)
+    for k in range(routes):
+        named = jnp.where(ids[k : k + 1, :] == expert, 1.0, named)
+    slot = jnp.dot(
+        named.astype(BF16), jnp.where(earlier, 1.0, 0.0).astype(BF16), preferred_element_type=F32
+    ).astype(jnp.int32)
+    slot = jnp.where(named > 0.0, slot, -1)
+    taken = slot[:, None, :] == place
+    chosen = jnp.where(taken, 1.0, 0.0).reshape(experts * capacity, rows).astype(BF16)
+    reads[2].wait()
+    writes = []
+    for k in range(STEPS):
+        cols = pl.ds(k * (width // STEPS), width // STEPS)
+        out[:, cols] = jnp.dot(chosen, tokens[:, cols], preferred_element_type=F32).astype(BF16)
+        writes.append(pltpu.make_async_copy(out.at[:, cols], out_ref.at[:, cols], sems.at[4 + k]))
+        writes[-1].start()
+    reads[1].wait()
+    weight = jnp.zeros((experts, rows), F32)
+    for k in range(routes):
+        weight = jnp.where(ids[k : k + 1, :] == expert, weights[k : k + 1, :].astype(F32), weight)
+    combine[...] = jnp.where(taken, weight[:, None, :], 0.0).astype(BF16)
+    writes.append(pltpu.make_async_copy(combine, combine_ref, sems.at[3]))
+    writes[-1].start()
+    for copy in writes:
+        copy.wait()
 
 
 def dispatch_rows(expert_ids, route_weights, tokens, experts, capacity):
     rows, width = tokens.shape
     routes = expert_ids.shape[1]
-    small = pl.BlockSpec((routes, rows), lambda i: (0, 0))
     return pl.pallas_call(
         dispatch_kernel,
-        grid=(STEPS,),
         out_shape=(
             jax.ShapeDtypeStruct((experts * capacity, width), BF16),
             jax.ShapeDtypeStruct((experts, capacity, rows), BF16),
         ),
-        in_specs=[small, small, pl.BlockSpec((rows, width // STEPS), lambda i: (0, i))],
-        out_specs=(
-            pl.BlockSpec((experts * capacity, width // STEPS), lambda i: (0, i)),
-            pl.BlockSpec((experts, capacity, rows), lambda i: (0, 0, 0)),
-        ),
-        scratch_shapes=[pltpu.VMEM((experts * capacity, rows), BF16)],
+        in_specs=[IN_HBM] * 3,
+        out_specs=(IN_HBM, IN_HBM),
+        scratch_shapes=[
+            pltpu.VMEM((routes, rows), jnp.int32),
+            pltpu.VMEM((routes, rows), BF16),
+            pltpu.VMEM((rows, width), BF16),
+            pltpu.VMEM((experts * capacity, width), BF16),
+            pltpu.VMEM((experts, capacity, rows), BF16),
+            pltpu.SemaphoreType.DMA((4 + STEPS,)),
+        ],
         compiler_params=pltpu.CompilerParams(vmem_limit_bytes=60 * 2**20),
         cost_estimate=pl.CostEstimate(
             flops=2 * experts * capacity * rows * width,
@@ -77,10 +96,11 @@
 def hidden_kernel(x_ref, gate_ref, up_ref, out_ref, x_buf, weights, sems):
     rows, width = x_ref.shape
     units = gate_ref.shape[1]
-    depth = width // PIECES
-    copies = []
-    for k in range(PIECES):
-        part = pl.ds(k * depth, depth)
+    depth = width // sum(PIECES)
+    parts, copies = [], []
+    for k, share in enumerate(PIECES):
+        part = pl.ds(sum(PIECES[:k]) * depth, share * depth)
+        parts.append(part)
         copies.append(
             (
                 pltpu.make_async_copy(x_ref.at[:, part], x_buf.at[:, part], sems.at[2, k]),
@@ -96,10 +116,9 @@
         for copy in group:
             copy.start()
     total = jnp.zeros((rows, 2 * units), F32)
-    for k in range(PIECES):
+    for k, part in enumerate(parts):
         for copy in copies[k]:
             copy.wait()
-        part = pl.ds(k * depth, depth)
         total += jnp.dot(x_buf[:, part], weights[part, :], preferred_element_type=F32)
     gate, up = total[:, :units], total[:, units:]
     out_ref[...] = (gate / (1.0 + jnp.exp(-gate)) * up).astype(out_ref.dtype)
@@ -116,7 +135,7 @@
         scratch_shapes=[
             pltpu.VMEM((rows, width), BF16),
             pltpu.VMEM((width, 2 * units), BF16),
-            pltpu.SemaphoreType.DMA((3, PIECES)),
+            pltpu.SemaphoreType.DMA((3, len(PIECES))),
         ],
         compiler_params=pltpu.CompilerParams(vmem_limit_bytes=56 * 2**20),
         cost_estimate=pl.CostEstimate(

time: 121 us -> 121 us (level)
  no operation moved by 1% of the time
where the time goes in v6:
time: 121 us
  starting transfers between devices  45.6 us (38%)
  blocking collectives  43.5 us (36%)
  waiting for transfers between devices  18.7 us (15%)
  Pallas kernels  8.73 us (7%)
  local copies, waits for them, and re-layouts  3.16 us (3%)
    ppermute x7, starting transfers between devices, shift(): return lax.ppermute(x, axis, [(i, (i + by) % count) for i in range(count)])  27.3 us
    all_to_all x1, blocking collectives, per_device(): lax.all_to_all(expert_out.reshape(sources, capacity, quarter), 'expert',...  24.6 us
    all_gather x1, blocking collectives, per_device(): gathered = lax.all_gather(mine, 'etp')  18.8 us
    all_to_all x1, starting transfers between devices, per_device(): lax.all_to_all(outgoing.reshape(experts, capacity, width), 'expert', spli...  18.3 us
    ppermute x7, waiting for transfers between devices, shift(): return lax.ppermute(x, axis, [(i, (i + by) % count) for i in range(count)])  16.8 us
    pallas_call x1, Pallas kernels, hidden_units(): pl.pallas_call(hidden_kernel, out_shape=pltpu.VMEM((rows, units), BF16),...  4.66 us
    pallas_call x1, Pallas kernels, dispatch_rows(): pl.pallas_call(dispatch_kernel, out_shape=(jax.ShapeDtypeStruct((experts...  2.76 us
  transfers between devices with their start and end apart: 8, of which 3 were waited for; matrix products, arithmetic and copies ran while one was open for 3% of the time, Pallas kernels for 4%

profile of v6, /device:TPU:1, one launch (start us, length us, event | category | flops | bytes accessed | tf_op | source)
XLA Modules:
  0.0 120.7 jit_solution(12206777034927301709)
XLA Ops:
  0.0 2.8 %shard_map.64 = (bf16[256,4096]{1,0:T(8,128)(2,1)}, bf16[16,16,64]{2,1,0:T(8,128)(2,1)}) custom-call(s32[2,64]{1,0:T(2,128)} %bitcast.27, bf16[2,64]{1,0:T(2,128)(2,1)} %bitcast.28, bf16[64,4096]{1,0:T(8,128)(2,1)} %tokens_ref.1), custom_call_target="tpu_custom_call" | custom-call | flops 134217728 | bytes 2621440 | tf_op jit(solution)/shard_map/pallas_call | solution.py:71
  2.8 18.3 %all-to-all-start = ((bf16[16,16,4096]{2,1,0:T(8,128)(2,1)}), bf16[16,16,4096]{2,1,0:T(8,128)(2,1)}, u32[]{:S(2)}, u32[]{:S(2)}) async-start(bf16[16,16,4096]{2,1,0:T(8,128)(2,1)} %bitcast.26), calls=%async_computation | async-start | bytes 4194304 | tf_op jit(solution)/shard_map/all_to_all | solution.py:218
  21.1 1.2 dynamic-slice_bitcast_fusion.1
  22.2 1.9 %collective-permute-start = (bf16[384,256]{1,0:T(8,128)(2,1)S(1)}, bf16[384,256]{1,0:T(8,128)(2,1)S(1)}, u32[]{:S(2)}, u32[]{:S(2)}) collective-permute-start(bf16[384,256]{1,0:T(8,128)(2,1)S(1)} %get-tuple-element.10), channel_id=1, source_target_pairs={{0,1},{1,2},{2,3},{3,0},{4,5},{5,6},{6,7},{7,4},{8,9},{9,10},{10,1... | collective-permute-start | bytes 589832 | tf_op jit(solution)/shard_map/ppermute | solution.py:20
  24.1 8.2 %collective-permute-start.1 = (bf16[384,256]{1,0:T(8,128)(2,1)S(1)}, bf16[384,256]{1,0:T(8,128)(2,1)S(1)}, u32[]{:S(2)}, u32[]{:S(2)}) collective-permute-start(bf16[384,256]{1,0:T(8,128)(2,1)S(1)} %get-tuple-element.11), channel_id=1, source_target_pairs={{0,2},{1,3},{2,0},{3,1},{4,6},{5,7},{6,4},{7,5},{8,10},{9,11},{10,... | collective-permute-start | bytes 589832 | tf_op jit(solution)/shard_map/ppermute | solution.py:20
  32.3 1.9 %collective-permute-start.2 = (bf16[384,256]{1,0:T(8,128)(2,1)S(1)}, bf16[384,256]{1,0:T(8,128)(2,1)S(1)}, u32[]{:S(2)}, u32[]{:S(2)}) collective-permute-start(bf16[384,256]{1,0:T(8,128)(2,1)S(1)} %get-tuple-element.9), channel_id=1, source_target_pairs={{0,3},{1,0},{2,1},{3,2},{4,7},{5,4},{6,5},{7,6},{8,11},{9,8},{10,9... | collective-permute-start | bytes 589832 | tf_op jit(solution)/shard_map/ppermute | solution.py:20
  34.3 1.2 dynamic-slice_bitcast_fusion.own
  35.5 0.0 collective-permute-done
  35.5 12.5 %collective-permute-done.1 = bf16[384,256]{1,0:T(8,128)(2,1)S(1)} collective-permute-done((bf16[384,256]{1,0:T(8,128)(2,1)S(1)}, bf16[384,256]{1,0:T(8,128)(2,1)S(1)}, u32[]{:S(2)}, u32[]{:S(2)}) %collective-permute-start.1) | collective-permute-done | bytes 196640 | tf_op jit(solution)/shard_map/ppermute | solution.py:20
  48.0 4.3 %collective-permute-done.2 = bf16[384,256]{1,0:T(8,128)(2,1)S(1)} collective-permute-done((bf16[384,256]{1,0:T(8,128)(2,1)S(1)}, bf16[384,256]{1,0:T(8,128)(2,1)S(1)}, u32[]{:S(2)}, u32[]{:S(2)}) %collective-permute-start.2) | collective-permute-done | bytes 196640 | tf_op jit(solution)/shard_map/ppermute | solution.py:20
  52.3 3.4 %collective-permute-start.3 = (bf16[1152,256]{1,0:T(8,128)(2,1)S(1)}, bf16[1152,256]{1,0:T(8,128)(2,1)S(1)}, u32[]{:S(2)}, u32[]{:S(2)}) collective-permute-start(bf16[1152,256]{1,0:T(8,128)(2,1)S(1)} %constant_dynamic-update-slice_fusion.fetched), channel_id=1, source_target_pairs={{0,128},{64,192},{128,256},{192,320},{256,384},{320,448},{384,512}... | collective-permute-start | bytes 1769480 | tf_op jit(solution)/shard_map/ppermute | solution.py:20
  55.7 4.5 %collective-permute-start.4 = (bf16[1152,256]{1,0:T(8,128)(2,1)S(1)}, bf16[1152,256]{1,0:T(8,128)(2,1)S(1)}, u32[]{:S(2)}, u32[]{:S(2)}) collective-permute-start(bf16[1152,256]{1,0:T(8,128)(2,1)S(1)} %constant_dynamic-update-slice_fusion.fetched), channel_id=1, source_target_pairs={{0,896},{64,960},{128,0},{192,64},{256,128},{320,192},{384,256},{4... | collective-permute-start | bytes 1769480 | tf_op jit(solution)/shard_map/ppermute | solution.py:20
  60.2 0.8 fusion.1
  61.0 1.9 %collective-permute-start.5 = (bf16[1152,128]{1,0:T(8,128)(2,1)}, bf16[1152,128]{1,0:T(8,128)(2,1)S(1)}, u32[]{:S(2)}, u32[]{:S(2)}) collective-permute-start(bf16[1152,128]{1,0:T(8,128)(2,1)} %get-tuple-element.13), channel_id=1, source_target_pairs={{0,256},{64,320},{128,384},{192,448},{256,512},{320,576},{384,640}... | collective-permute-start | bytes 884744 | tf_op jit(solution)/shard_map/ppermute | solution.py:20
  62.9 5.5 %collective-permute-start.6 = (bf16[1152,128]{1,0:T(8,128)(2,1)S(1)}, bf16[1152,128]{1,0:T(8,128)(2,1)S(1)}, u32[]{:S(2)}, u32[]{:S(2)}) collective-permute-start(bf16[1152,128]{1,0:T(8,128)(2,1)S(1)} %get-tuple-element.12), channel_id=1, source_target_pairs={{0,768},{64,832},{128,896},{192,960},{256,0},{320,64},{384,128},{4... | collective-permute-start | bytes 884744 | tf_op jit(solution)/shard_map/ppermute | solution.py:20
  68.4 1.9 %all-to-all-done = bf16[16,16,4096]{2,1,0:T(8,128)(2,1)} async-done(((bf16[16,16,4096]{2,1,0:T(8,128)(2,1)}), bf16[16,16,4096]{2,1,0:T(8,128)(2,1)}, u32[]{:S(2)}, u32[]{:S(2)}) %all-to-all-start) | async-done | bytes 2097184 | tf_op jit(solution)/shard_map/all_to_all | solution.py:218
  70.3 4.7 %shard_map.65 = bf16[256,384]{1,0:T(8,128)(2,1)S(1)} custom-call(bf16[256,4096]{1,0:T(8,128)(2,1)} %bitcast.3.x_ref, bf16[4096,384]{1,0:T(8,128)(2,1)} %bitcast.24, bf16[4096,384]{1,0:T(8,128)(2,1)} %bitcast.25), custom_call_target="tpu_custom_call" | custom-call | flops 1610612736 | bytes 8585216 | tf_op jit(solution)/shard_map/pallas_call | solution.py:130
  74.9 0.0 copy-start
  74.9 18.8 %all-gather = bf16[1024,384]{1,0:T(8,128)(2,1)S(1)} all-gather(bf16[256,384]{1,0:T(8,128)(2,1)S(1)} %shard_map.65), channel_id=2, replica_groups=mesh['dp'=16,'expert'=16,'etp'=4] {'etp'}, dimensions={0}, use_global_device_ids=true | all-gather | bytes 983040 | tf_op jit(solution)/shard_map/all_gather | solution.py:223
  93.8 0.0 collective-permute-done.5.low
  93.8 0.0 collective-permute-done.6.high
  93.8 0.0 collective-permute-done.3.left
  93.8 0.0 collective-permute-done.4.right
  93.8 1.3 %shard_map.66 = bf16[256,1024]{1,0:T(8,128)(2,1)S(1)} custom-call(bf16[4,256,384]{2,1,0:T(8,128)(2,1)S(1)} %bitcast.22, bf16[384,1024]{1,0:T(8,128)(2,1)S(1)} %dynamic-slice_bitcast_fusion.own, bf16[1152,256]{1,0:T(8,128)(2,1)S(1)} %constant_dynamic-update-slice_fusion.fetched, bf16[1152,256]{1,0:T(8,128)(2,1)S(1)} %collective-permute-done.3.left, ...), custom_call_target="tpu_custom_call" | custom-call | flops 805306368 | bytes 4456448 | tf_op jit(solution)/shard_map/pallas_call | solution.py:175
  95.1 24.6 %all_to_all.10 = bf16[16,16,1024]{2,1,0:T(8,128)(2,1)S(1)} all-to-all(bf16[16,16,1024]{2,1,0:T(8,128)(2,1)S(1)} %bitcast.23), channel_id=1, replica_groups=mesh['dp'=16,'expert'=16,'etp'=4] {'expert'}, dimensions={0} | all-to-all | bytes 1048576 | tf_op jit(solution)/shard_map/all_to_all | solution.py:225
  119.8 0.0 copy-done
  119.8 0.9 fusion
  (3 shorter events, 0.0 us)
Async XLA Ops:
  2.8 67.5 %all-to-all-start = ((bf16[16,16,4096]{2,1,0:T(8,128)(2,1)}), bf16[16,16,4096]{2,1,0:T(8,128)(2,1)}, u32[]{:S(2)}, u32[]{:S(2)}) async-start(bf16[16,16,4096]{2,1,0:T(8,128)(2,1)} %bitcast.26), calls=%async_computation | async-start | bytes 4194304 | tf_op jit(solution)/shard_map/all_to_all | solution.py:218
  22.2 13.2 %collective-permute-start = (bf16[384,256]{1,0:T(8,128)(2,1)S(1)}, bf16[384,256]{1,0:T(8,128)(2,1)S(1)}, u32[]{:S(2)}, u32[]{:S(2)}) collective-permute-start(bf16[384,256]{1,0:T(8,128)(2,1)S(1)} %get-tuple-element.10), channel_id=1, source_target_pairs={{0,1},{1,2},{2,3},{3,0},{4,5},{5,6},{6,7},{7,4},{8,9},{9,10},{10,1... | collective-permute-start | bytes 589832 | tf_op jit(solution)/shard_map/ppermute | solution.py:20
  24.1 23.8 %collective-permute-start.1 = (bf16[384,256]{1,0:T(8,128)(2,1)S(1)}, bf16[384,256]{1,0:T(8,128)(2,1)S(1)}, u32[]{:S(2)}, u32[]{:S(2)}) collective-permute-start(bf16[384,256]{1,0:T(8,128)(2,1)S(1)} %get-tuple-element.11), channel_id=1, source_target_pairs={{0,2},{1,3},{2,0},{3,1},{4,6},{5,7},{6,4},{7,5},{8,10},{9,11},{10,... | collective-permute-start | bytes 589832 | tf_op jit(solution)/shard_map/ppermute | solution.py:20
  32.3 19.9 %collective-permute-start.2 = (bf16[384,256]{1,0:T(8,128)(2,1)S(1)}, bf16[384,256]{1,0:T(8,128)(2,1)S(1)}, u32[]{:S(2)}, u32[]{:S(2)}) collective-permute-start(bf16[384,256]{1,0:T(8,128)(2,1)S(1)} %get-tuple-element.9), channel_id=1, source_target_pairs={{0,3},{1,0},{2,1},{3,2},{4,7},{5,4},{6,5},{7,6},{8,11},{9,8},{10,9... | collective-permute-start | bytes 589832 | tf_op jit(solution)/shard_map/ppermute | solution.py:20
  52.3 41.5 %collective-permute-start.3 = (bf16[1152,256]{1,0:T(8,128)(2,1)S(1)}, bf16[1152,256]{1,0:T(8,128)(2,1)S(1)}, u32[]{:S(2)}, u32[]{:S(2)}) collective-permute-start(bf16[1152,256]{1,0:T(8,128)(2,1)S(1)} %constant_dynamic-update-slice_fusion.fetched), channel_id=1, source_target_pairs={{0,128},{64,192},{128,256},{192,320},{256,384},{320,448},{384,512}... | collective-permute-start | bytes 1769480 | tf_op jit(solution)/shard_map/ppermute | solution.py:20
  55.7 38.1 %collective-permute-start.4 = (bf16[1152,256]{1,0:T(8,128)(2,1)S(1)}, bf16[1152,256]{1,0:T(8,128)(2,1)S(1)}, u32[]{:S(2)}, u32[]{:S(2)}) collective-permute-start(bf16[1152,256]{1,0:T(8,128)(2,1)S(1)} %constant_dynamic-update-slice_fusion.fetched), channel_id=1, source_target_pairs={{0,896},{64,960},{128,0},{192,64},{256,128},{320,192},{384,256},{4... | collective-permute-start | bytes 1769480 | tf_op jit(solution)/shard_map/ppermute | solution.py:20
  61.0 32.8 %collective-permute-start.5 = (bf16[1152,128]{1,0:T(8,128)(2,1)}, bf16[1152,128]{1,0:T(8,128)(2,1)S(1)}, u32[]{:S(2)}, u32[]{:S(2)}) collective-permute-start(bf16[1152,128]{1,0:T(8,128)(2,1)} %get-tuple-element.13), channel_id=1, source_target_pairs={{0,256},{64,320},{128,384},{192,448},{256,512},{320,576},{384,640}... | collective-permute-start | bytes 884744 | tf_op jit(solution)/shard_map/ppermute | solution.py:20
  62.9 30.9 %collective-permute-start.6 = (bf16[1152,128]{1,0:T(8,128)(2,1)S(1)}, bf16[1152,128]{1,0:T(8,128)(2,1)S(1)}, u32[]{:S(2)}, u32[]{:S(2)}) collective-permute-start(bf16[1152,128]{1,0:T(8,128)(2,1)S(1)} %get-tuple-element.12), channel_id=1, source_target_pairs={{0,768},{64,832},{128,896},{192,960},{256,0},{320,64},{384,128},{4... | collective-permute-start | bytes 884744 | tf_op jit(solution)/shard_map/ppermute | solution.py:20
  74.9 44.8 %copy-start = (bf16[16,16,64]{2,1,0:T(8,128)(2,1)S(1)}, bf16[16,16,64]{2,1,0:T(8,128)(2,1)}, u32[]{:S(2)}) copy-start(bf16[16,16,64]{2,1,0:T(8,128)(2,1)} %get-tuple-element.7) | copy-start | bytes 98308
